TPU v7x, 128 devices: a whole 4x4x4 slice. The times are simulated.
128 devices in a mesh: rep: 1, tp: 16 (over z, y), ep: 8 (over x, core).
Axes of the slice: x: 4, y: 4, z: 4, core: 2. Of those that a mesh axis runs over, the one named last changes fastest.
Arguments:
- x_in: bfloat16 [8192, 1536], P(('rep', 'ep'))
- route_ids: int32 [2, 8192, 8], P(None, ('rep', 'ep'))
- gate_vals: float32 [2, 8192, 8], P(None, ('rep', 'ep'))
- w_gate: bfloat16 [2, 64, 1536, 512], P(None, ('rep', 'ep'), None, 'tp')
- w_up: bfloat16 [2, 64, 1536, 512], P(None, ('rep', 'ep'), None, 'tp')
- w_down: bfloat16 [2, 64, 512, 1536], P(None, ('rep', 'ep'), 'tp')
- old_map: int32 [2, 64], replicated
- move_src: int32 [2, 32], replicated
- move_dst: int32 [2, 32], replicated
Outputs:
- output 1: bfloat16 [8192, 1536], P(('rep', 'ep'))
- output 2: bfloat16 [2, 64, 1536, 512], P(None, ('rep', 'ep'), None, 'tp')
- output 3: bfloat16 [2, 64, 1536, 512], P(None, ('rep', 'ep'), None, 'tp')
- output 4: bfloat16 [2, 64, 512, 1536], P(None, ('rep', 'ep'), 'tp')
All inputs are finite; a program needn't handle non-finite values.
Results may differ from a plain program's by a relative error of at most 0.0073047.
Values are sent between devices in bfloat16 or wider.
A program may use at most 1 GiB of HBM per device.

v0:
```python
import jax
import jax.numpy as jnp
from jax import lax
from jax.sharding import PartitionSpec as P


def slot_table(slot_map, all_slots):
    return jax.ops.segment_min(jnp.arange(all_slots, dtype=jnp.int32), slot_map, num_segments=all_slots)


def moe_layer(hidden, layer_ids, layer_gates, w_gate, w_up, w_down, first_slot, group_size, capacity):
    tokens, top_k = layer_ids.shape
    local_slots = w_gate.shape[0]
    model_dim = hidden.shape[1]
    all_slots = group_size * local_slots
    slot_flat = first_slot[layer_ids.reshape(-1)]
    one_hot = (slot_flat[:, None] == jnp.arange(all_slots, dtype=jnp.int32)[None, :]).astype(jnp.int32)
    slot_rank = jnp.sum(jnp.cumsum(one_hot, axis=0) * one_hot, axis=1) - 1
    dest_row = slot_flat * capacity + slot_rank
    row_token = jnp.full((all_slots * capacity,), tokens, jnp.int32).at[dest_row].set(jnp.arange(tokens * top_k, dtype=jnp.int32) // top_k)
    padded = jnp.concatenate([hidden, jnp.zeros((1, model_dim), hidden.dtype)], axis=0)
    send_rows = padded[row_token].reshape(group_size, local_slots, capacity, model_dim)
    recv_rows = lax.all_to_all(send_rows, 'ep', 0, 2, tiled=True).reshape(local_slots, group_size * capacity, model_dim)
    gate_acc = jnp.einsum('scd,sdf->scf', recv_rows, w_gate, preferred_element_type=jnp.float32)
    up_acc = jnp.einsum('scd,sdf->scf', recv_rows, w_up, preferred_element_type=jnp.float32)
    hidden_act = (jax.nn.silu(gate_acc) * up_acc).astype(jnp.bfloat16)
    part_out = jnp.einsum('scf,sfd->scd', hidden_act, w_down, preferred_element_type=jnp.float32)
    expert_out = lax.psum(part_out, 'tp').astype(jnp.bfloat16)
    returned = lax.all_to_all(expert_out.reshape(1, local_slots, group_size * capacity, model_dim), 'ep', 2, 0, tiled=True)
    back_rows = returned.reshape(all_slots * capacity, model_dim)[dest_row].reshape(tokens, top_k, model_dim)
    mixture = jnp.sum(layer_gates[:, :, None] * back_rows, axis=1)
    return (hidden.astype(jnp.float32) + mixture).astype(jnp.bfloat16)


def outgoing_rows(weights, move_src, my_rank, local_slots):
    owns_src = ((move_src // local_slots) == my_rank)[:, None, None]
    src_local = move_src % local_slots
    return tuple(jnp.where(owns_src, w_arr[src_local], jnp.zeros((), w_arr.dtype)) for w_arr in weights)


def install(weights, incoming, move_dst, my_rank, local_slots):
    my_slots = my_rank * local_slots + jnp.arange(local_slots, dtype=jnp.int32)
    dst_match = my_slots[:, None] == move_dst[None, :]
    has_move = jnp.any(dst_match, axis=1)[:, None, None]
    move_pick = jnp.argmax(dst_match, axis=1)
    return tuple(jnp.where(has_move, inc_arr[move_pick], w_arr) for inc_arr, w_arr in zip(incoming, weights))


def solution(mesh):
    group_size = mesh.shape['ep']
    row_spec = P(('rep', 'ep'), None)
    layer_spec = P(None, ('rep', 'ep'), None)
    col_spec = P(None, ('rep', 'ep'), None, 'tp')
    down_spec = P(None, ('rep', 'ep'), 'tp', None)
    map_spec = P(None, None)

    def device_step(x_in, route_ids, gate_vals, w_gate, w_up, w_down, old_map, move_src, move_dst):
        local_slots = w_gate.shape[1]
        tokens, top_k = route_ids.shape[1], route_ids.shape[2]
        all_slots = group_size * local_slots
        capacity = 2 * tokens * top_k // all_slots
        my_rank = lax.axis_index('ep')
        hidden = x_in
        new_sets = []
        for layer_idx in range(2):
            weights = (w_gate[layer_idx], w_up[layer_idx], w_down[layer_idx])
            incoming = lax.psum(outgoing_rows(weights, move_src[layer_idx], my_rank, local_slots), 'ep')
            weights = install(weights, incoming, move_dst[layer_idx], my_rank, local_slots)
            new_map = old_map[layer_idx].at[move_dst[layer_idx]].set(old_map[layer_idx][move_src[layer_idx]])
            first_slot = slot_table(new_map, all_slots)
            hidden = moe_layer(hidden, route_ids[layer_idx], gate_vals[layer_idx], weights[0], weights[1], weights[2], first_slot, group_size, capacity)
            new_sets.append(weights)
        return (hidden, jnp.stack([new_sets[0][0], new_sets[1][0]]), jnp.stack([new_sets[0][1], new_sets[1][1]]), jnp.stack([new_sets[0][2], new_sets[1][2]]))

    return jax.shard_map(device_step, mesh=mesh, in_specs=(row_spec, layer_spec, layer_spec, col_spec, col_spec, down_spec, map_spec, map_spec, map_spec), out_specs=(row_spec, col_spec, col_spec, down_spec), check_vma=False)
```

profile of v0, /device:TPU:1, one launch (start us, length us, event | category | flops | bytes accessed | tf_op | source)
XLA Modules:
  0.0 7807.6 jit_solution(3257321851850350213)
XLA Ops:
  18.8 4.5 compare_select_fusion.12
  23.3 5.8 compare_reduce_fusion.113
  29.1 36.0 select_select_fusion.1
  65.1 1.6 fusion.8
  66.7 34.5 reduce-window.14
  101.2 1.7 slice_reduce_fusion.1
  103.8 1.8 fusion.7
  105.7 30.5 scatter_custom_fusion.2
  136.2 2.1 concatenate.6
  138.3 73.6 gather_fusion.1
  211.9 9.9 all-to-all-start
  222.6 2.4 gather_fusion.13
  226.4 2.4 gather_fusion.11
  230.3 2.4 gather_fusion.15
  232.7 2.6 gather_fusion.6
  235.3 2.5 gather_fusion.4
  237.9 2.6 gather_fusion.2
  240.5 4.0 broadcast_select_fusion.3
  244.6 1.9 broadcast_select_fusion
  248.6 3.7 broadcast_select_fusion.1
  253.7 3.1 broadcast_select_fusion.4
  259.0 621.6 %all-reduce.7.cloned.1.call-done = (bf16[32,32,1536]{2,1,0:T(8,128)(2,1)}, bf16[32,32,1536]{2,1,0:T(8,128)(2,1)}, bf16[32,1536,32]{1,2,0:T(8,128)(2,1)}, bf16[32...) async-done(((bf16[32,32,1536]{2,1,0:T(8,128)(2,1)}, bf16[32,32,1536]{2,1,0:T(8,128)(2,1)}, bf16[32,1536,32]{1,2,0:T(8,128)(2,1)}, ...) | async-done | bytes 18874384 | tf_op jit(solution)/shard_map/psum | solution.py:67
  880.6 3.4 gather_fusion.7
  884.0 2.5 gather_fusion.3
  886.5 2.8 gather_fusion.5
  889.3 52.4 all-to-all-done
  941.7 33.8 copy.39
  975.6 21.9 fusion.20
  997.5 55.0 fusion.16
  1052.5 2125.3 %all-reduce.8 = bf16[8,2048,1536]{2,1,0:T(8,128)(2,1)} all-reduce(f32[8,2048,1536]{2,1,0:T(8,128)} %fusion.16), channel_id=1, replica_groups=mesh['rep'=1,'tp'=16,'ep'=8] {'tp'}, use_global_device_ids=true, to_apply=%region_11.12 | all-reduce | flops 25165824 | bytes 150994944 | tf_op jit(solution)/shard_map/psum | solution.py:28
  3177.9 45.5 copy.40
  3223.4 13.1 all-to-all-start.1
  3244.2 4.4 compare_select_fusion.6
  3248.6 5.8 compare_reduce_fusion.56
  3254.4 36.1 select_select_fusion
  3290.5 1.6 fusion.9
  3292.1 34.0 reduce-window.16
  3326.1 1.7 slice_reduce_fusion
  3328.8 1.8 fusion.5
  3330.6 30.7 scatter_custom_fusion.5
  3361.4 418.1 %all-to-all-done.1 = bf16[1,8,2048,1536]{3,1,0,2:T(8,128)(2,1)} async-done(((bf16[1,8,2048,1536]{3,1,0,2:T(8,128)(2,1)}), bf16[1,8,2048,1536]{3,1,0,2:T(8,128)(2,1)}, u32[]{:S(2)}, u32[]{:S(2)}) %all-to-all-start.1) | async-done | bytes 50331680 | tf_op jit(solution)/shard_map/all_to_all | solution.py:29
  3779.5 34.4 copy.41
  3813.9 175.0 %gather_fusion.8 = bf16[8192,1536]{1,0:T(8,128)(2,1)} fusion(bf16[16384,1536]{1,0:T(8,128)(2,1)} %bitcast.318, s32[8192]{0:T(1024)S(1)} %broadcast_clamp_fusion.1), kind=kCustom, calls=%fused_computation.8 | custom fusion | bytes 50364416 | tf_op jit(solution)/shard_map/gather | solution.py:30
  3988.9 66.1 fusion.1
  4054.9 3.8 add_convert_fusion.1
  4058.8 1.7 copy-done.7
  4060.6 73.6 gather_fusion.10
  4134.2 9.8 all-to-all-start.2
  4144.8 3.4 gather_fusion.16
  4148.2 2.5 gather_fusion.12
  4150.7 2.5 gather_fusion.14
  4153.2 533.8 %all-to-all-done.2 = bf16[8,8,256,1536]{3,2,1,0:T(8,128)(2,1)} async-done(((bf16[8,8,256,1536]{3,2,1,0:T(8,128)(2,1)}), bf16[8,8,256,1536]{3,2,1,0:T(8,128)(2,1)}, u32[]{:S(2)}, u32[]{:S(2)}) %all-to-all-start.2) | async-done | bytes 50331680 | tf_op jit(solution)/shard_map/all_to_all | solution.py:23
  4687.0 33.8 copy.44
  4720.8 22.0 fusion.14
  4742.8 55.0 fusion.10
  4797.8 2115.9 %all-reduce.9 = bf16[8,2048,1536]{2,1,0:T(8,128)(2,1)} all-reduce(f32[8,2048,1536]{2,1,0:T(8,128)} %fusion.10), channel_id=1, replica_groups=mesh['rep'=1,'tp'=16,'ep'=8] {'tp'}, use_global_device_ids=true, to_apply=%region_24.25 | all-reduce | flops 25165824 | bytes 150994944 | tf_op jit(solution)/shard_map/psum | solution.py:28
  6913.8 45.5 copy.45
  6959.3 17.9 all-to-all-start.3
  6978.2 1.7 bitcast_select_fusion.1
  6984.3 535.7 %all-to-all-done.3 = bf16[1,8,2048,1536]{3,1,0,2:T(8,128)(2,1)} async-done(((bf16[1,8,2048,1536]{3,1,0,2:T(8,128)(2,1)}), bf16[1,8,2048,1536]{3,1,0,2:T(8,128)(2,1)}, u32[]{:S(2)}, u32[]{:S(2)}) %all-to-all-start.3) | async-done | bytes 50331680 | tf_op jit(solution)/shard_map/all_to_all | solution.py:29
  7520.0 34.0 copy.46
  7554.0 175.0 %gather_fusion.17 = bf16[8192,1536]{1,0:T(8,128)(2,1)} fusion(bf16[16384,1536]{1,0:T(8,128)(2,1)} %bitcast.319, s32[8192]{0:T(1024)S(1)} %broadcast_clamp_fusion), kind=kCustom, calls=%fused_computation.17 | custom fusion | bytes 50364416 | tf_op jit(solution)/shard_map/gather | solution.py:30
  7729.0 66.1 fusion
  7795.1 5.5 add_convert_fusion
  (137 shorter events, 37.0 us)
Async XLA Ops:
  16.9 88.8 %copy-start.28 = (s32[8192]{0:T(1024)}, s32[8192]{0:T(1024)S(1)}, u32[]{:S(2)}) copy-start(s32[8192]{0:T(1024)S(1)} %add_select_fusion) | copy-start | bytes 98308
  105.7 30.5 copy-start.21
  211.9 9.9 copy-start.36
  211.9 9.9 copy-start.37
  211.9 10.5 copy-start.13
  211.9 729.8 %all-to-all-start = ((bf16[8,8,256,1536]{3,2,1,0:T(8,128)(2,1)}), bf16[8,8,256,1536]{3,2,1,0:T(8,128)(2,1)}, u32[]{:S(2)}, u32[]{:S(2)}) async-start(bf16[8,8,256,1536]{3,2,1,0:T(8,128)(2,1)} %bitcast.326), calls=%async_computation | async-start | bytes 100663296 | tf_op jit(solution)/shard_map/all_to_all | solution.py:23
  221.8 658.8 %all-reduce.7.cloned.1.call-start = ((), (), s32[]{:S(2)}) async-start(), calls=%async_computation.4 | async-start | bytes 37748736 | tf_op jit(solution)/shard_map/psum | solution.py:67
  237.9 2.6 copy-start.33
  240.5 4.1 copy-start.16
  244.6 3.0 copy-start.1
  244.6 4.0 copy-start.2
  248.6 3.7 copy-start.3
  248.6 5.1 copy-start.4
  256.8 0.7 copy-start.34
  257.4 629.0 %copy-start.29 = (s32[8]{0:T(128)}, s32[8]{0:T(128)S(1)}, u32[]{:S(2)}) copy-start(s32[8]{0:T(128)S(1)} %iota_add_fusion) | copy-start | bytes 100
  257.4 629.0 %copy-start.31 = (s32[32]{0:T(128)}, s32[32]{0:T(128)S(1)}, u32[]{:S(2)}) copy-start(s32[32]{0:T(128)S(1)} %get-tuple-element.161) | copy-start | bytes 388
  259.0 738.5 %copy-start.19 = (pred[8]{0:T(512)(128)(4,1)}, pred[8]{0:T(512)(128)(4,1)S(1)}, u32[]{:S(2)}) copy-start(pred[8]{0:T(512)(128)(4,1)S(1)} %get-tuple-element.123) | copy-start | bytes 28
  886.5 89.0 %copy-start.9 = (bf16[8,1536,32]{1,2,0:T(8,128)(2,1)}, bf16[8,1536,32]{1,2,0:T(8,128)(2,1)S(1)}, u32[]{:S(2)}) copy-start(bf16[8,1536,32]{1,2,0:T(8,128)(2,1)S(1)} %gather_fusion.3) | copy-start | bytes 2359300
  889.3 108.2 %copy-start.5 = (bf16[8,1536,32]{1,2,0:T(8,128)(2,1)}, bf16[8,1536,32]{1,2,0:T(8,128)(2,1)S(1)}, u32[]{:S(2)}) copy-start(bf16[8,1536,32]{1,2,0:T(8,128)(2,1)S(1)} %gather_fusion.5) | copy-start | bytes 2359300
  975.5 22.0 copy-start.11
  3223.4 13.2 copy-start.24
  3223.4 13.7 copy-start.27
  3223.4 15.3 copy-start
  3223.4 16.1 copy-start.35
  3223.4 556.1 %all-to-all-start.1 = ((bf16[1,8,2048,1536]{3,1,0,2:T(8,128)(2,1)}), bf16[1,8,2048,1536]{3,1,0,2:T(8,128)(2,1)}, u32[]{:S(2)}, u32[]{:S(2)}) async-start(bf16[1,8,2048,1536]{3,1,0,2:T(8,128)(2,1)} %copy.40), calls=%async_computation.1 | async-start | bytes 100663296 | tf_op jit(solution)/shard_map/all_to_all | solution.py:29
  3328.0 33.3 copy-start.22
  3330.6 483.2 %copy-start.25 = (s32[8192,1]{0,1:T(1,128)}, s32[8192,1]{0,1:T(1,128)S(1)}, u32[]{:S(2)}) copy-start(s32[8192,1]{0,1:T(1,128)S(1)} %compare_select_fusion) | copy-start | bytes 98308
  3988.9 66.1 copy-start.17
  4058.7 1.7 copy-start.7
  4134.2 9.9 copy-start.30
  4134.2 9.9 copy-start.32
  4134.2 552.7 %all-to-all-start.2 = ((bf16[8,8,256,1536]{3,2,1,0:T(8,128)(2,1)}), bf16[8,8,256,1536]{3,2,1,0:T(8,128)(2,1)}, u32[]{:S(2)}, u32[]{:S(2)}) async-start(bf16[8,8,256,1536]{3,2,1,0:T(8,128)(2,1)} %bitcast.327), calls=%async_computation.2 | async-start | bytes 100663296 | tf_op jit(solution)/shard_map/all_to_all | solution.py:23
  4687.0 33.8 copy-start.18
  4720.8 22.0 copy-start.12
  6959.2 17.9 copy-start.23
  6959.2 18.9 copy-start.26
  6959.3 18.9 copy-start.20
  6959.3 560.8 %all-to-all-start.3 = ((bf16[1,8,2048,1536]{3,1,0,2:T(8,128)(2,1)}), bf16[1,8,2048,1536]{3,1,0,2:T(8,128)(2,1)}, u32[]{:S(2)}, u32[]{:S(2)}) async-start(bf16[1,8,2048,1536]{3,1,0,2:T(8,128)(2,1)} %copy.45), calls=%async_computation.3 | async-start | bytes 100663296 | tf_op jit(solution)/shard_map/all_to_all | solution.py:29
  6978.2 3.1 copy-start.6
  6978.2 3.1 copy-start.10
  6978.2 3.1 copy-start.14
  6978.2 3.0 copy-start.15
  7729.0 66.1 copy-start.8
Sparse Core Ops, SparseCore 0:
  256.9 623.6 all-reduce.6
where the time goes:
time: 7830 us; the launch traced here: 7810 us
  blocking collectives  4240 us (54%)
  waiting for transfers between devices  2160 us (28%)
  local copies, waits for them, and re-layouts  847 us (11%)
  other arithmetic  338 us (4%)
  matrix products  154 us (2%)
    psum x2, blocking collectives, moe_layer(): expert_out = lax.psum(part_out, 'tp').astype(jnp.bfloat16)  4240 us
    all_to_all x2, waiting for transfers between devices, moe_layer(): lax.all_to_all(expert_out.reshape(1, local_slots, group_size * capacity,...  954 us
    psum x1, waiting for transfers between devices, device_step(): lax.psum(outgoing_rows(weights, move_src[layer_idx], my_rank, local_slots...  622 us
    all_to_all x2, waiting for transfers between devices, moe_layer(): lax.all_to_all(send_rows, 'ep', 0, 2, tiled=True)  586 us
    gather x2, local copies, waits for them, and re-layouts, moe_layer(): returned.reshape(all_slots * capacity, model_dim)[dest_row]  350 us
  transfers between devices with their start and end apart: 5, of which 5 were waited for; matrix products, arithmetic and copies ran while one was open for 2% of the time, Pallas kernels for 0%

commit v1 on v0

v1 whole, which is shorter than its diff:
```python
import functools

import jax
import jax.numpy as jnp
from jax import lax
from jax.experimental import pallas as pl
from jax.experimental.pallas import tpu as pltpu
from jax.sharding import PartitionSpec as P

EXPERTS = 40
F32 = jnp.float32
BF16 = jnp.bfloat16


def combine_kernel(cap, group, slots, first_ref, back_ref, rank_ref, gate_ref, res_ref, out_ref, acc_ref):
    tokens = rank_ref.shape[1]
    feats = out_ref.shape[0]
    acc_ref[...] = res_ref[...].astype(F32)
    row_iota = lax.broadcasted_iota(jnp.int32, (cap, tokens), 0)

    def step(expert, carry):
        slot = first_ref[expert]
        owner = slot // slots
        pair = 2 * (slot - owner * slots)
        rows = back_ref[pl.ds(pair, 2), owner].reshape(cap, feats)
        pick = (rank_ref[pl.ds(expert, 1), :] == row_iota).astype(BF16)
        chosen = lax.dot_general(rows, pick, (((0,), (0,)), ((), ())), preferred_element_type=F32)
        acc_ref[...] += gate_ref[pl.ds(expert, 1), :] * chosen
        return carry

    lax.fori_loop(0, EXPERTS, step, 0)
    out_ref[...] = acc_ref[...].astype(BF16)


def combine(first_slot, back, rank, gate, residual, cap, group, slots):
    feats, tokens = residual.shape
    return pl.pallas_call(
        functools.partial(combine_kernel, cap, group, slots),
        out_shape=jax.ShapeDtypeStruct((feats, tokens), BF16),
        in_specs=[pl.BlockSpec(memory_space=pltpu.SMEM)] + [pl.BlockSpec(memory_space=pltpu.VMEM)] * 4,
        out_specs=pl.BlockSpec(memory_space=pltpu.VMEM),
        scratch_shapes=[pltpu.VMEM((feats, tokens), F32)],
        cost_estimate=pl.CostEstimate(flops=2 * EXPERTS * cap * 256 * tokens, bytes_accessed=8 << 20, transcendentals=0),
    )(first_slot, back, rank, gate, residual)


def solution(mesh):
    group = mesh.shape['ep']
    cols = mesh.shape['tp']
    row_spec = P(('rep', 'ep'), None)
    layer_spec = P(None, ('rep', 'ep'), None)
    col_spec = P(None, ('rep', 'ep'), None, 'tp')
    down_spec = P(None, ('rep', 'ep'), 'tp', None)
    map_spec = P(None, None)

    def device_step(x_in, route_ids, gate_vals, w_gate, w_up, w_down, old_map, move_src, move_dst):
        layers, slots, width, part = w_gate.shape
        tokens, top_k = route_ids.shape[1], route_ids.shape[2]
        all_slots = group * slots
        cap = 2 * tokens * top_k // all_slots
        half = cap // 2
        feats = width // cols
        ep = lax.axis_index('ep')
        tp = lax.axis_index('tp')
        packed = jnp.stack([jnp.swapaxes(w_gate, 2, 3), jnp.swapaxes(w_up, 2, 3), w_down], axis=2)

        full = []
        for layer in range(layers):
            send = jnp.repeat(packed[layer], 2, axis=0)
            got = lax.all_to_all(send, 'tp', 0, 0, tiled=True)
            full.append([got[:, k].reshape(cols * part, width) for k in range(3)])

        tables = []
        expert_ids = jnp.arange(EXPERTS, dtype=jnp.int32)
        before = (jnp.arange(tokens)[:, None] < jnp.arange(tokens)[None, :]).astype(BF16)
        for layer in range(layers):
            ids = route_ids[layer].T
            match = ids[None, :, :] == expert_ids[:, None, None]
            taken = jnp.any(match, axis=1)
            gate = jnp.sum(jnp.where(match, gate_vals[layer].T[None], 0.0), axis=1)
            rank = jnp.dot(taken.astype(BF16), before, preferred_element_type=F32).astype(jnp.int32)
            rank = jnp.where(taken, rank, -1)
            slot_ids = jnp.arange(all_slots, dtype=jnp.int32)
            holds = old_map[layer][None, :] == expert_ids[:, None]
            first = jnp.min(jnp.where(holds, slot_ids[None, :], all_slots - 1), axis=1)
            my_slots = jnp.arange(group, dtype=jnp.int32) * slots + tp // 2
            serves = first[:, None] == my_slots[None, :]
            picked = jnp.sum(jnp.where(serves[:, :, None], rank[:, None, :] + 1, 0), axis=0) - 1
            row = jnp.arange(half, dtype=jnp.int32) + half * (tp % 2)
            pick = (picked[:, None, :] == row[None, :, None]).astype(BF16)
            tables.append((rank, gate, first, pick.reshape(group * half, tokens)))

        hidden = x_in
        hidden_dim = 0
        residual = lax.dynamic_slice_in_dim(x_in, tp * feats, feats, axis=1).T
        for layer in range(layers):
            rank, gate, first, pick = tables[layer]
            send = lax.dot_general(pick, hidden, (((1,), (hidden_dim,)), ((), ())), preferred_element_type=F32).astype(BF16)
            rows = lax.all_to_all(send.reshape(group, half, width), 'ep', 0, 0, tiled=True).reshape(group * half, width)
            wg, wu, wd = full[layer]
            gate_acc = lax.dot_general(rows, wg, (((1,), (1,)), ((), ())), preferred_element_type=F32)
            up_acc = lax.dot_general(rows, wu, (((1,), (1,)), ((), ())), preferred_element_type=F32)
            act = (jax.nn.silu(gate_acc) * up_acc).astype(BF16)
            out = jnp.dot(act, wd, preferred_element_type=F32).astype(BF16)
            back = lax.all_to_all(out.reshape(group, half, width), 'ep', 0, 0, tiled=True)
            back = back.reshape(group, half, cols, feats).transpose(2, 0, 1, 3)
            back = lax.all_to_all(back, 'tp', 0, 0, tiled=True)
            residual = combine(first, back, rank, gate, residual, cap, group, slots)
            hidden = lax.all_gather(residual, 'tp', axis=0, tiled=True)
            hidden_dim = 1
        y_out = hidden.T

        pieces = group // layers
        depth = 3 * part // pieces
        send = packed.reshape(layers, slots, pieces, depth, width).transpose(0, 2, 1, 3, 4).reshape(group, slots, depth, width)
        held = lax.all_to_all(send, 'ep', 0, 0, tiled=True).reshape(all_slots, depth, width)
        source = jnp.arange(all_slots, dtype=jnp.int32)
        my_layer = ep // pieces
        source = source.at[move_dst[my_layer]].set(move_src[my_layer])
        held = held[source].reshape(group, slots, depth, width)
        got = lax.all_to_all(held, 'ep', 0, 0, tiled=True)
        new = got.reshape(layers, pieces, slots, depth, width).transpose(0, 2, 1, 3, 4).reshape(layers, slots, 3, part, width)
        return y_out, jnp.swapaxes(new[:, :, 0], 2, 3), jnp.swapaxes(new[:, :, 1], 2, 3), new[:, :, 2]

    return jax.shard_map(device_step, mesh=mesh, in_specs=(row_spec, layer_spec, layer_spec, col_spec, col_spec, down_spec, map_spec, map_spec, map_spec), out_specs=(row_spec, col_spec, col_spec, down_spec), check_vma=False)
```

time: 7830 us -> 654 us (0.08)
  blocking collectives: 4240 us -> 142 us
  waiting for transfers between devices: 2160 us -> 313 us
  local copies, waits for them, and re-layouts: 847 us -> 60.6 us
  other arithmetic: 338 us -> 8.76 us
  matrix products: 154 us -> 40 us
    psum x2 -> x0, blocking collectives: 4240 us -> none  [moe_layer(): expert_out = lax.psum(part_out, 'tp').astype(jnp.bfloat16)]
    all_to_all x4 -> x7, waiting for transfers between devices: 1540 us -> 228 us  [the longest x2 73.5 us: device_step(): back = lax.all_to_all(back, 'tp', 0, 0, tiled=True)]
    psum x1 -> x0, waiting for transfers between devices: 622 us -> none  [device_step(): lax.psum(outgoing_rows(weights, move_src[layer_idx], my_rank, local_slots...]
    gather x26 -> x1, local copies, waits for them, and re-layouts: 536 us -> 5.36 us  [device_step(): held = held[source].reshape(group, slots, depth, width)]
    all_to_all x0 -> x3, blocking collectives: none -> 142 us  [the longest x2 82.9 us: device_step(): lax.all_to_all(out.reshape(group, half, width), 'ep', 0, 0, tiled=True)]
    reduce_sum x4, other arithmetic: 136 us -> 2.49 us  [the longest x2 2.18 us: device_step(): gate = jnp.sum(jnp.where(match, gate_vals[layer].T[None], 0.0), axis=1)]
    all_to_all x4 -> x2, local copies, waits for them, and re-layouts: 136 us -> 10.8 us  [device_step(): back = lax.all_to_all(back, 'tp', 0, 0, tiled=True)]
    dot_general x4 -> x8, matrix products: 154 us -> 40 us  [the longest x2 16.3 us: device_step(): out = jnp.dot(act, wd, preferred_element_type=F32).astype(BF16)]
  transfers between devices with their start and end apart: 5 -> 9, of which waited for: 5 -> 7; matrix products, arithmetic and copies ran while one was open for 2% -> 8% of each run, Pallas kernels for 0% -> 2%
where the time goes in v1:
time: 654 us; the launch traced here: 652 us
  waiting for transfers between devices  313 us (48%)
  blocking collectives  142 us (22%)
  local copies, waits for them, and re-layouts  60.6 us (9%)
  starting transfers between devices  46.2 us (7%)
  matrix products  40 us (6%)
  Pallas kernels  27.4 us (4%)
  between operations  14.4 us (2%)
  other arithmetic  8.76 us (1%)
    all_gather x2, waiting for transfers between devices, device_step(): hidden = lax.all_gather(residual, 'tp', axis=0, tiled=True)  85.3 us
    all_to_all x2, blocking collectives, device_step(): lax.all_to_all(out.reshape(group, half, width), 'ep', 0, 0, tiled=True)  82.9 us
    all_to_all x2, waiting for transfers between devices, device_step(): back = lax.all_to_all(back, 'tp', 0, 0, tiled=True)  73.5 us
    all_to_all x2, waiting for transfers between devices, device_step(): lax.all_to_all(send.reshape(group, half, width), 'ep', 0, 0, tiled=True)  65.3 us
    all_to_all x1, blocking collectives, device_step(): got = lax.all_to_all(held, 'ep', 0, 0, tiled=True)  58.7 us
    all_to_all x2, waiting for transfers between devices, device_step(): got = lax.all_to_all(send, 'tp', 0, 0, tiled=True)  55.3 us
    all_to_all x1, waiting for transfers between devices, device_step(): lax.all_to_all(send, 'ep', 0, 0, tiled=True)  33.9 us
    pallas_call x2, Pallas kernels, combine(): pl.pallas_call(functools.partial(combine_kernel, cap, group, slots), out_...  27.4 us
  transfers between devices with their start and end apart: 9, of which 7 were waited for; matrix products, arithmetic and copies ran while one was open for 8% of the time, Pallas kernels for 2%

profile of v1, /device:TPU:1, one launch (start us, length us, event | category | flops | bytes accessed | tf_op | source)
XLA Modules:
  0.0 652.4 jit_solution(13395327758090369298)
XLA Ops:
  7.2 0.0 copy-start
  7.2 2.8 pad_maximum_fusion
  10.0 2.1 slice_bitcast_fusion.1
  12.1 0.8 copy-done.2
  12.8 2.9 broadcast_in_dim.115
  15.8 8.8 %all-to-all-start.1 = ((bf16[16,3,32,1536]{3,2,1,0:T(8,128)(2,1)}), bf16[16,3,32,1536]{3,2,1,0:T(8,128)(2,1)}, u32[]{:S(2)}, u32[]{:S(2)}) async-start(bf16[16,3,32,1536]{3,2,1,0:T(8,128)(2,1)} %bitcast.106), calls=%async_computation.1 | async-start | bytes 9437184 | tf_op jit(solution)/shard_map/all_to_all | solution.py:70
  24.6 0.1 select_reduce_fusion.4
  24.8 0.0 copy-start.7
  24.8 0.0 copy-start.8
  24.8 1.0 fusion.2
  25.8 0.1 broadcast_compare_fusion
  25.8 1.1 broadcast_add_fusion
  26.9 0.2 select_reduce_fusion.2
  27.1 1.1 broadcast_add_fusion.1
  28.1 0.2 select_reduce_fusion.3
  28.3 2.3 bitcast_compare_fusion
  30.7 0.0 copy-done.7
  30.7 4.8 convolution_convert_fusion.3
  35.4 55.3 %all-to-all-done.1 = bf16[16,3,32,1536]{3,2,1,0:T(8,128)(2,1)} async-done(((bf16[16,3,32,1536]{3,2,1,0:T(8,128)(2,1)}), bf16[16,3,32,1536]{3,2,1,0:T(8,128)(2,1)}, u32[]{:S(2)}, u32[]{:S(2)}) %all-to-all-start.1) | async-done | bytes 4718624 | tf_op jit(solution)/shard_map/all_to_all | solution.py:70
  90.8 7.7 %all-to-all-start = ((bf16[8,128,1536]{2,1,0:T(8,128)(2,1)}), bf16[8,128,1536]{2,1,0:T(8,128)(2,1)}, u32[]{:S(2)}, u32[]{:S(2)}) async-start(bf16[8,128,1536]{2,1,0:T(8,128)(2,1)} %bitcast.118), calls=%async_computation | async-start | bytes 6291456 | tf_op jit(solution)/shard_map/all_to_all | solution.py:99
  98.5 4.7 fusion.14
  103.2 32.7 %all-to-all-done = bf16[8,128,1536]{2,1,0:T(8,128)(2,1)} async-done(((bf16[8,128,1536]{2,1,0:T(8,128)(2,1)}), bf16[8,128,1536]{2,1,0:T(8,128)(2,1)}, u32[]{:S(2)}, u32[]{:S(2)}) %all-to-all-start) | async-done | bytes 3145760 | tf_op jit(solution)/shard_map/all_to_all | solution.py:99
  135.9 5.5 fusion.15
  141.4 8.6 %convolution_convert_fusion.2 = bf16[1024,1536]{1,0:T(8,128)(2,1)} fusion(bf16[512,1536]{1,0:T(8,128)(2,1)} %bitcast.125, f32[1024,512]{1,0:T(8,128)} %fusion.15, bf16[1024,1536]{1,0:T(8,128)(2,1)} %bitcast.10, bf16[512,1536]{1,0:T(8,128)(2,1)} %bitcast.124), kind=kOutput, calls=%fused_computation.10 | convolution fusion | flops 3225944064 | bytes 11534336 | tf_op jit(solution)/shard_map/dot_general | solution.py:104
  150.0 4.7 copy.42
  154.7 41.8 %all_to_all.50 = bf16[8,128,1536]{1,2,0:T(8,128)(2,1)S(1)} all-to-all(bf16[8,128,1536]{1,2,0:T(8,128)(2,1)} %copy.42), channel_id=1, replica_groups=mesh['rep'=1,'tp'=16,'ep'=8] {'ep'}, dimensions={0} | all-to-all | bytes 6291456 | tf_op jit(solution)/shard_map/all_to_all | solution.py:105
  196.5 2.0 copy.43
  198.5 6.0 all-to-all-start.3
  204.5 0.2 all-gather.3.cloned.1.call-start
  204.7 0.1 constant_dynamic-slice_fusion.2
  204.9 0.8 copy.52
  205.7 1.1 select_reduce_fusion.1.gate_ref
  206.8 38.1 %all-to-all-done.3 = bf16[16,8,128,96]{2,3,1,0:T(8,128)(2,1)} async-done(((bf16[16,8,128,96]{2,3,1,0:T(8,128)(2,1)}), bf16[16,8,128,96]{2,3,1,0:T(8,128)(2,1)}, u32[]{:S(2)}, u32[]{:S(2)}) %all-to-all-start.3) | async-done | bytes 3145760 | tf_op jit(solution)/shard_map/all_to_all | solution.py:107
  244.9 6.0 copy.45.back_ref
  250.9 13.8 %shard_map.120.res_ref = bf16[96,1024]{1,0:T(8,128)(2,1)} custom-call(s32[40]{0:T(128)} %copy-done.8, bf16[16,8,128,96]{3,2,1,0:T(8,128)(2,1)} %copy.45.back_ref, s32[40,1024]{1,0:T(8,128)} %get-tuple-element.46.rank_ref, f32[40,1024]{1,0:T(8,128)} %select_reduce_fusion.1.gate_ref, bf16[96,1024]{1,0:T(8,128)(2,1)} %bitcast.130), custom_call_target="tpu_custom_call" | custom-call | flops 5368709120 | bytes 8388608 | tf_op jit(solution)/shard_map/pallas_call | solution.py:37
  264.7 0.0 all-gather.3.cloned.1.call-update
  264.7 2.8 broadcast_in_dim.118
  267.5 6.4 all-to-all-start.5
  274.0 85.3 %all-gather.3.cloned.1.call-done = bf16[1536,1024]{1,0:T(8,128)(2,1)} async-done(((bf16[96,1024]{1,0:T(8,128)(2,1)}), bf16[1536,1024]{1,0:T(8,128)(2,1)}) %all-gather.3.cloned.1.call-update) | async-done | bytes 3145744 | tf_op jit(solution)/shard_map/all_gather | solution.py:109
  359.3 6.7 %convolution_convert_fusion.1 = bf16[1024,1536]{1,0:T(8,128)(2,1)} fusion(pred[1024,1024]{1,0:T(32,128)(4,1)S(1)} %copy-done.4, bf16[1536,1024]{1,0:T(8,128)(2,1)} %all-gather.3.cloned.1.call-done), kind=kOutput, calls=%fused_computation.9 | convolution fusion | flops 3222798336 | bytes 7340032 | tf_op jit(solution)/shard_map/dot_general | solution.py:98
  366.0 0.0 all-to-all-done.5
  366.0 4.3 all-to-all-start.4
  370.3 4.7 fusion.13
  375.0 32.6 %all-to-all-done.4 = bf16[8,128,1536]{2,1,0:T(8,128)(2,1)S(1)} async-done(((bf16[8,128,1536]{2,1,0:T(8,128)(2,1)}), bf16[8,128,1536]{2,1,0:T(8,128)(2,1)S(1)}, u32[]{:S(2)}, u32[]{:S(2)}) %all-to-all-start.4) | async-done | bytes 3145760 | tf_op jit(solution)/shard_map/all_to_all | solution.py:99
  407.6 4.6 fusion.16
  412.2 7.7 %convolution_convert_fusion = bf16[1024,1536]{1,0:T(8,128)(2,1)} fusion(bf16[512,1536]{1,0:T(8,128)(2,1)} %bitcast.127, f32[1024,512]{1,0:T(8,128)} %fusion.16, bf16[1024,1536]{1,0:T(8,128)(2,1)S(1)} %bitcast.116, bf16[512,1536]{1,0:T(8,128)(2,1)} %bitcast.126), kind=kOutput, calls=%fused_computation.8 | convolution fusion | flops 3225944064 | bytes 11534336 | tf_op jit(solution)/shard_map/dot_general | solution.py:104
  419.9 3.5 copy.46
  423.3 41.0 %all_to_all.51 = bf16[8,128,1536]{1,2,0:T(8,128)(2,1)S(1)} all-to-all(bf16[8,128,1536]{1,2,0:T(8,128)(2,1)S(1)} %copy.46), channel_id=1, replica_groups=mesh['rep'=1,'tp'=16,'ep'=8] {'ep'}, dimensions={0} | all-to-all | bytes 6291456 | tf_op jit(solution)/shard_map/all_to_all | solution.py:105
  464.4 2.0 copy.47
  466.4 4.4 all-to-all-start.7
  470.8 5.0 copy.49
  475.8 35.5 %all-to-all-done.7 = bf16[16,8,128,96]{2,3,1,0:T(8,128)(2,1)S(1)} async-done(((bf16[16,8,128,96]{2,3,1,0:T(8,128)(2,1)}), bf16[16,8,128,96]{2,3,1,0:T(8,128)(2,1)S(1)}, u32[]{:S(2)}, u32[]{:S(2)}) %all-to-all-start.7) | async-done | bytes 3145760 | tf_op jit(solution)/shard_map/all_to_all | solution.py:107
  511.3 8.4 %all-to-all-start.8 = ((bf16[8,8,24,1536]{3,2,1,0:T(8,128)(2,1)}), bf16[8,8,24,1536]{3,2,1,0:T(8,128)(2,1)}, u32[]{:S(2)}, u32[]{:S(2)}) async-start(bf16[8,8,24,1536]{3,2,1,0:T(8,128)(2,1)} %bitcast.107), calls=%async_computation.8 | async-start | bytes 9437184 | tf_op jit(solution)/shard_map/all_to_all | solution.py:116
  519.6 1.1 select_reduce_fusion.gate_ref
  520.7 4.7 copy.48.back_ref
  525.5 13.6 %shard_map.121 = bf16[96,1024]{1,0:T(8,128)(2,1)} custom-call(s32[40]{0:T(128)} %copy-done.7, bf16[16,8,128,96]{3,2,1,0:T(8,128)(2,1)} %copy.48.back_ref, s32[40,1024]{1,0:T(8,128)} %get-tuple-element.48.rank_ref, f32[40,1024]{1,0:T(8,128)} %select_reduce_fusion.gate_ref, bf16[96,1024]{1,0:T(8,128)(2,1)} %shard_map.120.res_ref), custom_call_target="tpu_custom_call" | custom-call | flops 5368709120 | bytes 8388608 | tf_op jit(solution)/shard_map/pallas_call | solution.py:37
  539.1 0.0 all-gather.5.cloned.1.call-update
  539.2 0.7 scatter_fusion
  539.9 33.9 %all-to-all-done.8 = bf16[8,8,24,1536]{3,2,1,0:T(8,128)(2,1)} async-done(((bf16[8,8,24,1536]{3,2,1,0:T(8,128)(2,1)}), bf16[8,8,24,1536]{3,2,1,0:T(8,128)(2,1)}, u32[]{:S(2)}, u32[]{:S(2)}) %all-to-all-start.8) | async-done | bytes 4718624 | tf_op jit(solution)/shard_map/all_to_all | solution.py:116
  573.9 5.4 gather_fusion
  579.2 58.7 %all_to_all.52 = bf16[8,8,24,1536]{3,2,1,0:T(8,128)(2,1)S(1)} all-to-all(bf16[8,8,24,1536]{3,2,1,0:T(8,128)(2,1)} %bitcast.110), channel_id=1, replica_groups=mesh['rep'=1,'tp'=16,'ep'=8] {'ep'}, dimensions={0} | all-to-all | bytes 9437184 | tf_op jit(solution)/shard_map/all_to_all | solution.py:121
  638.0 0.6 copy.50
  638.5 2.3 slice_bitcast_fusion.2
  640.8 4.8 copy.51
  (34 shorter events, 0.1 us)
Async XLA Ops:
  7.2 23.5 %copy-start = (bf16[1024,1536]{1,0:T(8,128)(2,1)S(1)}, bf16[1024,1536]{1,0:T(8,128)(2,1)}, u32[]{:S(2)}) copy-start(bf16[1024,1536]{1,0:T(8,128)(2,1)} %param.9) | copy-start | bytes 9437188
  9.9 2.9 copy-start.2
  15.8 8.8 %copy-start.9 = (s32[2,64]{1,0:T(2,128)S(1)}, s32[2,64]{1,0:T(2,128)}, u32[]{:S(2)}) copy-start(s32[2,64]{1,0:T(2,128)} %param.15) | copy-start | bytes 1540
  15.8 9.0 %copy-start.5 = (s32[2,1024,8]{1,2,0:T(8,128)S(1)}, s32[2,1024,8]{1,2,0:T(8,128)}, u32[]{:S(2)}) copy-start(s32[2,1024,8]{1,2,0:T(8,128)} %param.10) | copy-start | bytes 196612
  15.8 75.0 %all-to-all-start.1 = ((bf16[16,3,32,1536]{3,2,1,0:T(8,128)(2,1)}), bf16[16,3,32,1536]{3,2,1,0:T(8,128)(2,1)}, u32[]{:S(2)}, u32[]{:S(2)}) async-start(bf16[16,3,32,1536]{3,2,1,0:T(8,128)(2,1)} %bitcast.106), calls=%async_computation.1 | async-start | bytes 9437184 | tf_op jit(solution)/shard_map/all_to_all | solution.py:70
  24.8 5.9 copy-start.7
  24.8 5.9 copy-start.8
  90.8 45.1 %all-to-all-start = ((bf16[8,128,1536]{2,1,0:T(8,128)(2,1)}), bf16[8,128,1536]{2,1,0:T(8,128)(2,1)}, u32[]{:S(2)}, u32[]{:S(2)}) async-start(bf16[8,128,1536]{2,1,0:T(8,128)(2,1)} %bitcast.118), calls=%async_computation | async-start | bytes 6291456 | tf_op jit(solution)/shard_map/all_to_all | solution.py:99
  198.5 7.2 %copy-start.6 = (f32[2,1024,8]{1,2,0:T(8,128)S(1)}, f32[2,1024,8]{1,2,0:T(8,128)}, u32[]{:S(2)}) copy-start(f32[2,1024,8]{1,2,0:T(8,128)} %param.11) | copy-start | bytes 196612
  198.5 46.4 %all-to-all-start.3 = ((bf16[16,8,128,96]{2,3,1,0:T(8,128)(2,1)}), bf16[16,8,128,96]{2,3,1,0:T(8,128)(2,1)}, u32[]{:S(2)}, u32[]{:S(2)}) async-start(bf16[16,8,128,96]{2,3,1,0:T(8,128)(2,1)} %copy.43), calls=%async_computation.3 | async-start | bytes 6291456 | tf_op jit(solution)/shard_map/all_to_all | solution.py:107
  204.5 154.8 %all-gather.3.cloned.1.call-start = ((), (), s32[]{:S(2)}) async-start(), calls=%async_computation.10 | async-start | bytes 3342336 | tf_op jit(solution)/shard_map/all_gather | solution.py:109
  250.9 13.8 %copy-start.3 = (bf16[8,3,32,1536]{3,2,1,0:T(8,128)(2,1)S(1)}, bf16[8,3,32,1536]{3,2,1,0:T(8,128)(2,1)}, u32[]{:S(2)}) copy-start(bf16[8,3,32,1536]{3,2,1,0:T(8,128)(2,1)} %get-tuple-element.34) | copy-start | bytes 7077892
  267.5 91.7 %copy-start.4 = (pred[1024,1024]{1,0:T(32,128)(4,1)S(1)}, pred[1024,1024]{1,0:T(32,128)(4,1)}, u32[]{:S(2)}) copy-start(pred[1024,1024]{1,0:T(32,128)(4,1)} %get-tuple-element.40) | copy-start | bytes 3145732
  267.5 98.4 %all-to-all-start.5 = ((bf16[16,3,32,1536]{3,2,1,0:T(8,128)(2,1)}), bf16[16,3,32,1536]{3,2,1,0:T(8,128)(2,1)}, u32[]{:S(2)}, u32[]{:S(2)}) async-start(bf16[16,3,32,1536]{3,2,1,0:T(8,128)(2,1)} %bitcast.108), calls=%async_computation.5 | async-start | bytes 9437184 | tf_op jit(solution)/shard_map/all_to_all | solution.py:70
  366.0 41.6 %all-to-all-start.4 = ((bf16[8,128,1536]{2,1,0:T(8,128)(2,1)}), bf16[8,128,1536]{2,1,0:T(8,128)(2,1)S(1)}, u32[]{:S(2)}, u32[]{:S(2)}) async-start(bf16[8,128,1536]{2,1,0:T(8,128)(2,1)} %bitcast.117), calls=%async_computation.4 | async-start | bytes 6291456 | tf_op jit(solution)/shard_map/all_to_all | solution.py:99
  466.4 44.9 %all-to-all-start.7 = ((bf16[16,8,128,96]{2,3,1,0:T(8,128)(2,1)}), bf16[16,8,128,96]{2,3,1,0:T(8,128)(2,1)S(1)}, u32[]{:S(2)}, u32[]{:S(2)}) async-start(bf16[16,8,128,96]{2,3,1,0:T(8,128)(2,1)} %copy.47), calls=%async_computation.7 | async-start | bytes 6291456 | tf_op jit(solution)/shard_map/all_to_all | solution.py:107
  511.3 62.6 %all-to-all-start.8 = ((bf16[8,8,24,1536]{3,2,1,0:T(8,128)(2,1)}), bf16[8,8,24,1536]{3,2,1,0:T(8,128)(2,1)}, u32[]{:S(2)}, u32[]{:S(2)}) async-start(bf16[8,8,24,1536]{3,2,1,0:T(8,128)(2,1)} %bitcast.107), calls=%async_computation.8 | async-start | bytes 9437184 | tf_op jit(solution)/shard_map/all_to_all | solution.py:116
  519.6 121.2 %all-gather.5.cloned.1.call-start = ((), (), s32[]{:S(2)}) async-start(), calls=%async_computation.11 | async-start | bytes 3342336 | tf_op jit(solution)/shard_map/all_gather | solution.py:109
  525.5 13.7 %copy-start.10 = (s32[2,32]{1,0:T(2,128)S(1)}, s32[2,32]{1,0:T(2,128)}, u32[]{:S(2)}) copy-start(s32[2,32]{1,0:T(2,128)} %param.17) | copy-start | bytes 772
  525.5 13.7 %copy-start.11 = (s32[2,32]{1,0:T(2,128)S(1)}, s32[2,32]{1,0:T(2,128)}, u32[]{:S(2)}) copy-start(s32[2,32]{1,0:T(2,128)} %param.16) | copy-start | bytes 772
  640.8 4.8 copy-start.1
Sparse Core Ops, SparseCore 0:
  264.8 94.4 all-gather.2
  539.2 45.6 all-gather.4

commit v2 on v1

v2 whole, which is shorter than its diff:
```python
import functools

import jax
import jax.numpy as jnp
from jax import lax
from jax.experimental import pallas as pl
from jax.experimental.pallas import tpu as pltpu
from jax.sharding import PartitionSpec as P

EXPERTS = 40
F32 = jnp.float32
BF16 = jnp.bfloat16
VMEM = pl.BlockSpec(memory_space=pltpu.VMEM)
SMEM = pl.BlockSpec(memory_space=pltpu.SMEM)
ANY = pl.BlockSpec(memory_space=pl.ANY)
MESH = pl.DeviceIdType.MESH


def exchange_kernel(group, cols, src_ref, dst_ref, send_sem, recv_sem):
    ep, tp = lax.axis_index('ep'), lax.axis_index('tp')
    me = ep * cols + tp
    total = group * cols

    def send(k, carry):
        to_ep = lax.rem(ep + lax.rem(k, group), group)
        to_tp = lax.rem(tp + k // group + lax.rem(k, group), cols)
        to = to_ep * cols + to_tp

        @pl.when(to != me)
        def _():
            pltpu.make_async_remote_copy(src_ref.at[to], dst_ref.at[me], send_sem, recv_sem, device_id={'tp': to_tp, 'ep': to_ep}, device_id_type=MESH).start()

        return carry

    lax.fori_loop(0, total, send, 0)
    pltpu.make_async_copy(src_ref.at[me], dst_ref.at[me], recv_sem).start()
    pltpu.make_async_copy(src_ref, dst_ref, recv_sem).wait()
    some = pl.ds(0, total - 1)
    pltpu.make_async_copy(src_ref.at[some], dst_ref.at[some], send_sem).wait()


def exchange(blocks, group, cols):
    return pl.pallas_call(
        functools.partial(exchange_kernel, group, cols),
        out_shape=jax.ShapeDtypeStruct(blocks.shape, blocks.dtype),
        in_specs=[ANY],
        out_specs=ANY,
        scratch_shapes=[pltpu.SemaphoreType.DMA, pltpu.SemaphoreType.DMA],
        compiler_params=pltpu.CompilerParams(has_side_effects=True),
        cost_estimate=pl.CostEstimate(flops=0, bytes_accessed=120 << 20, transcendentals=0),
    )(blocks)


def gather_kernel(cols, src_ref, dst_ref, send_sem, recv_sem):
    tp = lax.axis_index('tp')

    def send(k, carry):
        to = lax.rem(tp + k, cols)
        pltpu.make_async_remote_copy(src_ref, dst_ref.at[tp], send_sem, recv_sem, device_id={'tp': to}, device_id_type=MESH).start()
        return carry

    lax.fori_loop(1, cols, send, 0)
    pltpu.make_async_copy(src_ref, dst_ref.at[tp], recv_sem).start()
    pltpu.make_async_copy(dst_ref, dst_ref, recv_sem).wait()
    some = dst_ref.at[pl.ds(0, cols - 1)]
    pltpu.make_async_copy(some, some, send_sem).wait()


def gather_cols(block, cols):
    return pl.pallas_call(
        functools.partial(gather_kernel, cols),
        out_shape=jax.ShapeDtypeStruct((cols,) + block.shape, block.dtype),
        in_specs=[ANY],
        out_specs=ANY,
        scratch_shapes=[pltpu.SemaphoreType.DMA, pltpu.SemaphoreType.DMA],
        compiler_params=pltpu.CompilerParams(has_side_effects=True),
        cost_estimate=pl.CostEstimate(flops=0, bytes_accessed=120 << 20, transcendentals=0),
    )(block)


def expert_kernel(wide, rows_ref, mine_ref, other_ref, out_ref, down_ref):
    blocks = out_ref.shape[0]
    width = out_ref.shape[1]
    half = mine_ref.shape[0] * mine_ref.shape[2]

    def whole(k):
        return jnp.concatenate([mine_ref[:, k].reshape(half, width), other_ref[:, k].reshape(half, width)], axis=0)

    down_ref[...] = whole(2).T

    def step(i, carry):
        if wide:
            rows = jnp.concatenate([rows_ref[2 * i], rows_ref[2 * i + 1]], axis=1)
            dims = (((1,), (0,)), ((), ()))
        else:
            rows = jnp.concatenate([rows_ref[2 * i], rows_ref[2 * i + 1]], axis=0)
            dims = (((1,), (1,)), ((), ()))
        gate = lax.dot_general(whole(0), rows, dims, preferred_element_type=F32)
        up = lax.dot_general(whole(1), rows, dims, preferred_element_type=F32)
        act = (jax.nn.silu(gate) * up).astype(BF16)
        out = jnp.dot(down_ref[...], act, preferred_element_type=F32).astype(BF16)
        n = out_ref.shape[2]
        out_ref[2 * i] = out[:, :n]
        out_ref[2 * i + 1] = out[:, n:]
        return carry

    lax.fori_loop(0, blocks // 2, step, 0)


def run_expert(rows, mine, other, wide, width, half):
    blocks = rows.shape[0]
    ffn = 2 * mine.shape[0] * mine.shape[2]
    return pl.pallas_call(
        functools.partial(expert_kernel, wide),
        out_shape=jax.ShapeDtypeStruct((blocks, width, half), BF16),
        in_specs=[VMEM] * 3,
        out_specs=VMEM,
        scratch_shapes=[pltpu.VMEM((width, ffn), BF16)],
        cost_estimate=pl.CostEstimate(flops=6 * blocks * half * width * ffn, bytes_accessed=12 << 20, transcendentals=0),
    )(rows, mine, other)


def combine_kernel(cap, slots, cols, last, first_ref, next_ref, back_ref, rank_ref, gate_ref, nrank_ref, res_ref, out_ref, send_ref, acc_ref):
    tokens = rank_ref.shape[1]
    half = cap // 2
    acc_ref[...] = res_ref[...].astype(F32)
    row_iota = lax.broadcasted_iota(jnp.int32, (cap, tokens), 0)

    def step(expert, carry):
        slot = first_ref[expert]
        plane = slot // cols
        block = 2 * plane * cols + slot - plane * cols
        rows = jnp.concatenate([back_ref[block], back_ref[block + cols]], axis=1)
        pick = (rank_ref[pl.ds(expert, 1), :] == row_iota).astype(BF16)
        chosen = jnp.dot(rows, pick, preferred_element_type=F32)
        acc_ref[...] += gate_ref[pl.ds(expert, 1), :] * chosen
        return carry

    lax.fori_loop(0, EXPERTS, step, 0)
    out_ref[...] = acc_ref[...].astype(BF16)
    if last:
        return
    hidden = out_ref[...]

    def step2(expert, carry):
        slot = next_ref[expert]
        plane = slot // cols
        block = 2 * plane * cols + slot - plane * cols
        pick = (nrank_ref[pl.ds(expert, 1), :] == row_iota).astype(BF16)
        rows = lax.dot_general(hidden, pick, (((1,), (1,)), ((), ())), preferred_element_type=F32).astype(BF16)
        send_ref[block] = rows[:, :half]
        send_ref[block + cols] = rows[:, half:]
        return carry

    lax.fori_loop(0, EXPERTS, step2, 0)


def combine(first, nfirst, back, rank, gate, nrank, residual, cap, slots, cols, last):
    feats, tokens = residual.shape
    return pl.pallas_call(
        functools.partial(combine_kernel, cap, slots, cols, last),
        out_shape=(jax.ShapeDtypeStruct((feats, tokens), BF16), jax.ShapeDtypeStruct((8, 128) if last else back.shape, BF16)),
        in_specs=[SMEM] * 2 + [VMEM] * 5,
        out_specs=(VMEM, VMEM),
        scratch_shapes=[pltpu.VMEM((feats, tokens), F32)],
        cost_estimate=pl.CostEstimate(flops=2 * EXPERTS * cap * 256 * tokens, bytes_accessed=8 << 20, transcendentals=0),
    )(first, nfirst, back, rank, gate, nrank, residual)


def solution(mesh):
    group = mesh.shape['ep']
    cols = mesh.shape['tp']
    row_spec = P(('rep', 'ep'), None)
    layer_spec = P(None, ('rep', 'ep'), None)
    col_spec = P(None, ('rep', 'ep'), None, 'tp')
    down_spec = P(None, ('rep', 'ep'), 'tp', None)
    map_spec = P(None, None)

    def device_step(x_in, route_ids, gate_vals, w_gate, w_up, w_down, old_map, move_src, move_dst):
        layers, slots, width, part = w_gate.shape
        tokens, top_k = route_ids.shape[1], route_ids.shape[2]
        all_slots = group * slots
        cap = 2 * tokens * top_k // all_slots
        half = cap // 2
        feats = width // cols
        ep = lax.axis_index('ep')
        tp = lax.axis_index('tp')
        core = ep % 2
        partner = [(i, i ^ 1) for i in range(group)]
        packed = jnp.stack([jnp.swapaxes(w_gate, 2, 3), jnp.swapaxes(w_up, 2, 3), w_down], axis=2)

        full = []
        for layer in range(layers):
            cut = packed[layer].reshape(slots, 3, 2, part // 2, width)
            keep = lax.dynamic_index_in_dim(cut, core, 2, keepdims=False)
            give = lax.dynamic_index_in_dim(cut, 1 - core, 2, keepdims=False)
            take = lax.ppermute(give, 'ep', partner)
            send = jnp.where(core == 0, jnp.stack([keep, take]), jnp.stack([take, keep])).reshape(2 * slots, 3, part // 2, width)
            mine = lax.all_to_all(send, 'tp', 0, 0, tiled=True)
            full.append((mine, lax.ppermute(mine, 'ep', partner)))

        tables = []
        expert_ids = jnp.arange(EXPERTS, dtype=jnp.int32)
        before = (jnp.arange(tokens)[:, None] < jnp.arange(tokens)[None, :]).astype(BF16)
        for layer in range(layers):
            ids = route_ids[layer].T
            match = ids[None, :, :] == expert_ids[:, None, None]
            taken = jnp.any(match, axis=1)
            gate = jnp.sum(jnp.where(match, gate_vals[layer].T[None], 0.0), axis=1)
            rank = jnp.dot(taken.astype(BF16), before, preferred_element_type=F32).astype(jnp.int32)
            rank = jnp.where(taken, rank, -1)
            slot_ids = jnp.arange(all_slots, dtype=jnp.int32)
            holds = old_map[layer][None, :] == expert_ids[:, None]
            first = jnp.min(jnp.where(holds, slot_ids[None, :], all_slots - 1), axis=1)
            tables.append((rank, gate, first))

        rank, gate, first = tables[0]
        my_slots = jnp.arange(group // 2, dtype=jnp.int32) * cols + tp
        serves = first[:, None] == my_slots[None, :]
        picked = jnp.sum(jnp.where(serves[:, :, None], rank[:, None, :] + 1, 0), axis=0) - 1
        row = jnp.arange(cap, dtype=jnp.int32)
        pick = (picked[:, None, :] == row[None, :, None]).astype(BF16).reshape(group * half, tokens)
        send = jnp.dot(pick, x_in, preferred_element_type=F32).astype(BF16)
        rows = lax.all_to_all(send.reshape(group, half, width), 'ep', 0, 0, tiled=True)

        residual = lax.dynamic_slice_in_dim(x_in, tp * feats, feats, axis=1).T
        for layer in range(layers):
            last = layer == layers - 1
            rank, gate, first = tables[layer]
            nrank, _, nfirst = tables[layer if last else layer + 1]
            out = run_expert(rows, full[layer][0], full[layer][1], layer > 0, width, half)
            out = out.reshape(group, cols, feats, half).reshape(group * cols, feats, half)
            back = exchange(out, group, cols)
            residual, send = combine(first, nfirst, back, rank, gate, nrank, residual, cap, slots, cols, last)
            if not last:
                rows = exchange(send, group, cols).reshape(group, width, half)
        y_out = gather_cols(residual, cols).reshape(width, tokens).T

        pieces = group // layers
        depth = 3 * part // pieces
        send = packed.reshape(layers, slots, pieces, depth, width).transpose(0, 2, 1, 3, 4).reshape(group, slots, depth, width)
        held = lax.all_to_all(send, 'ep', 0, 0, tiled=True).reshape(all_slots, depth, width)
        source = jnp.arange(all_slots, dtype=jnp.int32)
        my_layer = ep // pieces
        source = source.at[move_dst[my_layer]].set(move_src[my_layer])
        held = held[source].reshape(group, slots, depth, width)
        got = lax.all_to_all(held, 'ep', 0, 0, tiled=True)
        new = got.reshape(layers, pieces, slots, depth, width).transpose(0, 2, 1, 3, 4).reshape(layers, slots, 3, part, width)
        return y_out, jnp.swapaxes(new[:, :, 0], 2, 3), jnp.swapaxes(new[:, :, 1], 2, 3), new[:, :, 2]

    return jax.shard_map(device_step, mesh=mesh, in_specs=(row_spec, layer_spec, layer_spec, col_spec, col_spec, down_spec, map_spec, map_spec, map_spec), out_specs=(row_spec, col_spec, col_spec, down_spec), check_vma=False)
```

time: 654 us -> 535 us (0.82)
  Pallas kernels: 27.4 us -> 318 us
  waiting for transfers between devices: 313 us -> 127 us
  blocking collectives: 142 us -> 0 us
  matrix products: 40 us -> 6.88 us
  local copies, waits for them, and re-layouts: 60.6 us -> 30.9 us
  between operations: 14.4 us -> 0.89 us
  starting transfers between devices: 46.2 us -> 38.2 us
    pallas_call x2 -> x8, Pallas kernels: 27.4 us -> 318 us  [the longest x3 195 us: exchange(): pl.pallas_call(functools.partial(exchange_kernel, group, cols), out_shape...]
    all_to_all x3 -> x0, blocking collectives: 142 us -> none  [the longest x2 82.9 us: device_step(): lax.all_to_all(out.reshape(group, half, width), 'ep', 0, 0, tiled=True)]
    all_gather x2 -> x0, waiting for transfers between devices: 85.3 us -> none  [device_step(): hidden = lax.all_gather(residual, 'tp', axis=0, tiled=True)]
    all_to_all x4 -> x3, waiting for transfers between devices: 129 us -> 51.2 us  [the longest x2 51.2 us: device_step(): mine = lax.all_to_all(send, 'tp', 0, 0, tiled=True)]
    all_to_all x2 -> x1, waiting for transfers between devices: 65.3 us -> 23.1 us  [device_step(): lax.all_to_all(send.reshape(group, half, width), 'ep', 0, 0, tiled=True)]
    dot_general x6 -> x1, matrix products: 37.9 us -> 4.75 us  [device_step(): send = jnp.dot(pick, x_in, preferred_element_type=F32).astype(BF16)]
    all_to_all x1, waiting for transfers between devices: 33.9 us -> 47.7 us  [device_step(): lax.all_to_all(send, 'ep', 0, 0, tiled=True)]
    all_to_all x2 -> x0, local copies, waits for them, and re-layouts: 10.8 us -> none  [device_step(): back = lax.all_to_all(back, 'tp', 0, 0, tiled=True)]
  transfers between devices with their start and end apart: 9 -> 9, of which waited for: 7 -> 6; matrix products, arithmetic and copies ran while one was open for 8% -> 6% of each run, Pallas kernels for 2% -> 59%
where the time goes in v2:
time: 535 us
  Pallas kernels  318 us (59%)
  waiting for transfers between devices  127 us (24%)
  starting transfers between devices  38.2 us (7%)
  local copies, waits for them, and re-layouts  30.9 us (6%)
  other arithmetic  12.8 us (2%)
  matrix products  6.88 us (1%)
    pallas_call x3, Pallas kernels, exchange(): pl.pallas_call(functools.partial(exchange_kernel, group, cols), out_shape...  195 us
    pallas_call x1, Pallas kernels, gather_cols(): pl.pallas_call(functools.partial(gather_kernel, cols), out_shape=jax.Shap...  62.4 us
    all_to_all x2, waiting for transfers between devices, device_step(): mine = lax.all_to_all(send, 'tp', 0, 0, tiled=True)  51.2 us
    all_to_all x1, waiting for transfers between devices, device_step(): lax.all_to_all(send, 'ep', 0, 0, tiled=True)  47.7 us
    pallas_call x2, Pallas kernels, combine(): pl.pallas_call(functools.partial(combine_kernel, cap, slots, cols, last),...  37 us
    pallas_call x2, Pallas kernels, run_expert(): pl.pallas_call(functools.partial(expert_kernel, wide), out_shape=jax.Shap...  23.1 us
    all_to_all x1, waiting for transfers between devices, device_step(): lax.all_to_all(send.reshape(group, half, width), 'ep', 0, 0, tiled=True)  23.1 us
    all_to_all x2, starting transfers between devices, device_step(): mine = lax.all_to_all(send, 'tp', 0, 0, tiled=True)  12.4 us
  transfers between devices with their start and end apart: 9, of which 6 were waited for; matrix products, arithmetic and copies ran while one was open for 6% of the time, Pallas kernels for 59%

profile of v2, /device:TPU:1, one launch (start us, length us, event | category | flops | bytes accessed | tf_op | source)
XLA Modules:
  0.0 534.7 jit_solution(2464684840867829501)
XLA Ops:
  0.6 0.0 copy-start
  0.7 0.9 slice_bitcast_fusion.7
  1.5 0.9 slice_bitcast_fusion.4
  2.4 0.4 fusion.3
  2.8 1.1 broadcast_add_fusion
  3.9 0.7 select_reduce_fusion.3
  4.6 0.0 copy-start.4
  4.6 0.1 broadcast_compare_fusion
  4.6 0.1 select_reduce_fusion.2
  4.8 0.7 bitcast_compare_fusion
  5.5 0.0 copy-done
  5.5 4.8 convolution_convert_fusion
  10.2 0.0 copy-done.4
  10.2 5.8 %all-to-all-start = ((bf16[8,128,1536]{2,1,0:T(8,128)(2,1)}), bf16[8,128,1536]{2,1,0:T(8,128)(2,1)}, u32[]{:S(2)}, u32[]{:S(2)}) async-start(bf16[8,128,1536]{2,1,0:T(8,128)(2,1)} %bitcast.96), calls=%async_computation | async-start | bytes 6291456 | tf_op jit(solution)/shard_map/all_to_all | solution.py:224
  16.0 2.6 pad_maximum_fusion
  18.6 0.0 copy-start.2
  18.6 1.9 fusion.11
  20.6 0.9 copy-done.2
  21.5 1.6 dynamic-slice_bitcast_fusion.3
  23.1 0.1 collective-permute-start
  23.1 2.7 collective-permute-done
  25.9 4.4 maximum_select_fusion
  30.3 23.1 %all-to-all-done.rows_ref = bf16[8,128,1536]{2,1,0:T(8,128)(2,1)} async-done(((bf16[8,128,1536]{2,1,0:T(8,128)(2,1)}), bf16[8,128,1536]{2,1,0:T(8,128)(2,1)}, u32[]{:S(2)}, u32[]{:S(2)}) %all-to-all-start) | async-done | bytes 3145760 | tf_op jit(solution)/shard_map/all_to_all | solution.py:224
  53.4 7.9 %all-to-all-start.1 = ((bf16[16,3,16,1536]{3,2,1,0:T(8,128)(2,1)}), bf16[16,3,16,1536]{3,2,1,0:T(8,128)(2,1)}, u32[]{:S(2)}, u32[]{:S(2)}) async-start(bf16[16,3,16,1536]{3,2,1,0:T(8,128)(2,1)} %bitcast.94), calls=%async_computation.1 | async-start | bytes 4718592 | tf_op jit(solution)/shard_map/all_to_all | solution.py:199
  61.2 4.9 copy.28
  66.2 26.4 %all-to-all-done.1.mine_ref = bf16[16,3,16,1536]{3,2,1,0:T(8,128)(2,1)} async-done(((bf16[16,3,16,1536]{3,2,1,0:T(8,128)(2,1)}), bf16[16,3,16,1536]{3,2,1,0:T(8,128)(2,1)}, u32[]{:S(2)}, u32[]{:S(2)}) %all-to-all-start.1) | async-done | bytes 2359328 | tf_op jit(solution)/shard_map/all_to_all | solution.py:199
  92.6 9.6 %all-to-all-start.3 = ((bf16[8,8,24,1536]{3,2,1,0:T(8,128)(2,1)}), bf16[8,8,24,1536]{3,2,1,0:T(8,128)(2,1)}, u32[]{:S(2)}, u32[]{:S(2)}) async-start(bf16[8,8,24,1536]{3,2,1,0:T(8,128)(2,1)} %bitcast.89), calls=%async_computation.3 | async-start | bytes 9437184 | tf_op jit(solution)/shard_map/all_to_all | solution.py:242
  102.2 1.8 dynamic-slice_bitcast_fusion.1
  104.0 0.2 collective-permute-start.2
  104.2 2.7 collective-permute-done.2
  106.9 1.8 maximum_select_fusion.1
  108.7 47.7 %all-to-all-done.3 = bf16[8,8,24,1536]{3,2,1,0:T(8,128)(2,1)} async-done(((bf16[8,8,24,1536]{3,2,1,0:T(8,128)(2,1)}), bf16[8,8,24,1536]{3,2,1,0:T(8,128)(2,1)}, u32[]{:S(2)}, u32[]{:S(2)}) %all-to-all-start.3) | async-done | bytes 4718624 | tf_op jit(solution)/shard_map/all_to_all | solution.py:242
  156.4 0.0 copy-start.5
  156.4 4.6 all-to-all-start.2
  161.0 0.0 copy-done.5
  161.0 0.0 copy-done.6
  161.1 0.7 scatter_fusion
  161.7 1.2 collective-permute-start.1
  162.9 5.3 gather_fusion
  168.2 24.9 %all-to-all-done.2.mine_ref = bf16[16,3,16,1536]{3,2,1,0:T(8,128)(2,1)} async-done(((bf16[16,3,16,1536]{3,2,1,0:T(8,128)(2,1)}), bf16[16,3,16,1536]{3,2,1,0:T(8,128)(2,1)}, u32[]{:S(2)}, u32[]{:S(2)}) %all-to-all-start.2) | async-done | bytes 2359328 | tf_op jit(solution)/shard_map/all_to_all | solution.py:199
  193.1 8.7 %all-to-all-start.4 = ((bf16[8,8,24,1536]{3,2,1,0:T(8,128)(2,1)}), bf16[8,8,24,1536]{3,2,1,0:T(8,128)(2,1)}, u32[]{:S(2)}, u32[]{:S(2)}) async-start(bf16[8,8,24,1536]{3,2,1,0:T(8,128)(2,1)} %bitcast.88), calls=%async_computation.4 | async-start | bytes 9437184 | tf_op jit(solution)/shard_map/all_to_all | solution.py:247
  201.8 0.2 collective-permute-start.3
  202.0 0.1 constant_dynamic-slice_fusion.2
  202.1 0.8 copy.30
  202.9 0.4 fusion.2
  203.4 0.0 copy-done.3
  203.4 1.5 select_reduce_fusion
  204.9 1.1 fusion.7.nrank_ref.rank_ref
  206.0 0.0 collective-permute-done.1.other_ref
  206.0 11.6 %shard_map.120 = bf16[8,1536,128]{2,1,0:T(8,128)(2,1)} custom-call(bf16[8,128,1536]{2,1,0:T(8,128)(2,1)} %all-to-all-done.rows_ref, bf16[16,3,16,1536]{3,2,1,0:T(8,128)(2,1)} %all-to-all-done.1.mine_ref, bf16[16,3,16,1536]{3,2,1,0:T(8,128)(2,1)} %collective-permute-done.1.other_ref), custom_call_target="tpu_custom_call" | custom-call | flops 4831838208 | bytes 12582912 | tf_op jit(solution)/shard_map/pallas_call | solution.py:113
  217.7 81.0 %shard_map.121.back_ref = bf16[128,96,128]{2,1,0:T(8,128)(2,1)} custom-call(bf16[128,96,128]{2,1,0:T(8,128)(2,1)} %bitcast.99), custom_call_target="tpu_custom_call" | custom-call | bytes 125829120 | tf_op jit(solution)/shard_map/pallas_call | solution.py:43
  298.7 25.0 %shard_map.122 = (bf16[96,1024]{1,0:T(8,128)(2,1)}, bf16[128,96,128]{2,1,0:T(8,128)(2,1)}) custom-call(s32[40]{0:T(128)} %copy-done.4, s32[40]{0:T(128)} %get-tuple-element.28.next_ref.first_ref, bf16[128,96,128]{2,1,0:T(8,128)(2,1)} %shard_map.121.back_ref, s32[40,1024]{1,0:T(8,128)} %get-tuple-element.26.rank_ref, f32[40,1024]{1,0:T(8,128)} %get-tuple-element.30.gate_ref, ...), custom_call_target="tpu_custom_call" | custom-call | flops 5368709120 | bytes 8388608 | tf_op jit(solution)/shard_map/pallas_call | solution.py:160
  323.7 56.2 %shard_map.123 = bf16[128,96,128]{2,1,0:T(8,128)(2,1)} custom-call(bf16[128,96,128]{2,1,0:T(8,128)(2,1)} %get-tuple-element.7.src_ref), custom_call_target="tpu_custom_call" | custom-call | bytes 125829120 | tf_op jit(solution)/shard_map/pallas_call | solution.py:43
  380.0 0.0 collective-permute-done.3.other_ref
  380.0 11.5 %shard_map.124 = bf16[8,1536,128]{2,1,0:T(8,128)(2,1)} custom-call(bf16[8,1536,128]{2,1,0:T(8,128)(2,1)} %bitcast.98, bf16[16,3,16,1536]{3,2,1,0:T(8,128)(2,1)} %all-to-all-done.2.mine_ref, bf16[16,3,16,1536]{3,2,1,0:T(8,128)(2,1)} %collective-permute-done.3.other_ref), custom_call_target="tpu_custom_call" | custom-call | flops 4831838208 | bytes 12582912 | tf_op jit(solution)/shard_map/pallas_call | solution.py:113
  391.5 57.8 %shard_map.125.back_ref = bf16[128,96,128]{2,1,0:T(8,128)(2,1)} custom-call(bf16[128,96,128]{2,1,0:T(8,128)(2,1)} %bitcast.100), custom_call_target="tpu_custom_call" | custom-call | bytes 125829120 | tf_op jit(solution)/shard_map/pallas_call | solution.py:43
  449.3 12.0 %shard_map.126 = (bf16[96,1024]{1,0:T(8,128)(2,1)}, bf16[8,128]{1,0:T(8,128)(2,1)}) custom-call(s32[40]{0:T(128)} %get-tuple-element.28.next_ref.first_ref, s32[40]{0:T(128)} %get-tuple-element.28.next_ref.first_ref, bf16[128,96,128]{2,1,0:T(8,128)(2,1)} %shard_map.125.back_ref, s32[40,1024]{1,0:T(8,128)} %fusion.7.nrank_ref.rank_ref, ...), custom_call_target="tpu_custom_call" | custom-call | flops 5368709120 | bytes 8388608 | tf_op jit(solution)/shard_map/pallas_call | solution.py:160
  461.2 62.4 %shard_map.127 = bf16[16,96,1024]{2,1,0:T(8,128)(2,1)} custom-call(bf16[96,1024]{1,0:T(8,128)(2,1)} %get-tuple-element.9.src_ref), custom_call_target="tpu_custom_call" | custom-call | bytes 125829120 | tf_op jit(solution)/shard_map/pallas_call | solution.py:70
  523.6 4.6 copy.27
  528.2 0.0 all-to-all-done.4
  528.2 2.8 copy.29
  531.1 0.0 copy-start.1
  531.1 2.5 slice_bitcast_fusion
  533.6 1.1 copy-done.1
  (12 shorter events, 0.1 us)
Async XLA Ops:
  0.6 4.8 copy-start
  4.6 5.7 %copy-start.4 = (s32[40]{0:T(128)}, s32[40]{0:T(128)S(1)}, u32[]{:S(2)}) copy-start(s32[40]{0:T(128)S(1)} %get-tuple-element.27.first_ref) | copy-start | bytes 484
  10.2 43.1 %all-to-all-start = ((bf16[8,128,1536]{2,1,0:T(8,128)(2,1)}), bf16[8,128,1536]{2,1,0:T(8,128)(2,1)}, u32[]{:S(2)}, u32[]{:S(2)}) async-start(bf16[8,128,1536]{2,1,0:T(8,128)(2,1)} %bitcast.96), calls=%async_computation | async-start | bytes 6291456 | tf_op jit(solution)/shard_map/all_to_all | solution.py:224
  18.6 2.9 copy-start.2
  23.1 2.8 collective-permute-start
  53.4 39.2 %all-to-all-start.1 = ((bf16[16,3,16,1536]{3,2,1,0:T(8,128)(2,1)}), bf16[16,3,16,1536]{3,2,1,0:T(8,128)(2,1)}, u32[]{:S(2)}, u32[]{:S(2)}) async-start(bf16[16,3,16,1536]{3,2,1,0:T(8,128)(2,1)} %bitcast.94), calls=%async_computation.1 | async-start | bytes 4718592 | tf_op jit(solution)/shard_map/all_to_all | solution.py:199
  92.6 63.8 %all-to-all-start.3 = ((bf16[8,8,24,1536]{3,2,1,0:T(8,128)(2,1)}), bf16[8,8,24,1536]{3,2,1,0:T(8,128)(2,1)}, u32[]{:S(2)}, u32[]{:S(2)}) async-start(bf16[8,8,24,1536]{3,2,1,0:T(8,128)(2,1)} %bitcast.89), calls=%async_computation.3 | async-start | bytes 9437184 | tf_op jit(solution)/shard_map/all_to_all | solution.py:242
  104.0 2.9 collective-permute-start.2
  156.4 4.6 copy-start.5
  156.4 4.6 copy-start.6
  156.4 36.7 %all-to-all-start.2 = ((bf16[16,3,16,1536]{3,2,1,0:T(8,128)(2,1)}), bf16[16,3,16,1536]{3,2,1,0:T(8,128)(2,1)}, u32[]{:S(2)}, u32[]{:S(2)}) async-start(bf16[16,3,16,1536]{3,2,1,0:T(8,128)(2,1)} %bitcast.92), calls=%async_computation.2 | async-start | bytes 4718592 | tf_op jit(solution)/shard_map/all_to_all | solution.py:199
  161.7 44.3 %collective-permute-start.1 = (bf16[16,3,16,1536]{3,2,1,0:T(8,128)(2,1)}, bf16[16,3,16,1536]{3,2,1,0:T(8,128)(2,1)}, u32[]{:S(2)}, u32[]{:S(2)}) collective-permute-start(bf16[16,3,16,1536]{3,2,1,0:T(8,128)(2,1)} %all-to-all-done.1.mine_ref), channel_id=1, source_target_pairs={{0,1},{1,0},{2,3},{3,2},{4,5},{5,4},{6,7},{7,6},{8,9},{9,8},{10,11... | collective-permute-start | bytes 7077896 | tf_op jit(solution)/shard_map/ppermute | solution.py:200
  193.1 10.3 %copy-start.3 = (f32[2,1024,8]{1,2,0:T(8,128)S(1)}, f32[2,1024,8]{1,2,0:T(8,128)}, u32[]{:S(2)}) copy-start(f32[2,1024,8]{1,2,0:T(8,128)} %param.11) | copy-start | bytes 196612
  193.1 335.1 %all-to-all-start.4 = ((bf16[8,8,24,1536]{3,2,1,0:T(8,128)(2,1)}), bf16[8,8,24,1536]{3,2,1,0:T(8,128)(2,1)}, u32[]{:S(2)}, u32[]{:S(2)}) async-start(bf16[8,8,24,1536]{3,2,1,0:T(8,128)(2,1)} %bitcast.88), calls=%async_computation.4 | async-start | bytes 9437184 | tf_op jit(solution)/shard_map/all_to_all | solution.py:247
  201.8 178.2 %collective-permute-start.3 = (bf16[16,3,16,1536]{3,2,1,0:T(8,128)(2,1)}, bf16[16,3,16,1536]{3,2,1,0:T(8,128)(2,1)}, u32[]{:S(2)}, u32[]{:S(2)}) collective-permute-start(bf16[16,3,16,1536]{3,2,1,0:T(8,128)(2,1)} %all-to-all-done.2.mine_ref), channel_id=1, source_target_pairs={{0,1},{1,0},{2,3},{3,2},{4,5},{5,4},{6,7},{7,6},{8,9},{9,8},{10,11... | collective-permute-start | bytes 7077896 | tf_op jit(solution)/shard_map/ppermute | solution.py:200
  531.1 3.6 copy-start.1

commit v3 on v1

v3 whole, which is shorter than its diff:
```python
import functools

import jax
import jax.numpy as jnp
from jax import lax
from jax.experimental import pallas as pl
from jax.experimental.pallas import tpu as pltpu
from jax.sharding import PartitionSpec as P

EXPERTS = 40
F32 = jnp.float32
BF16 = jnp.bfloat16
VMEM = pl.BlockSpec(memory_space=pltpu.VMEM)
SMEM = pl.BlockSpec(memory_space=pltpu.SMEM)
ANY = pl.BlockSpec(memory_space=pl.ANY)
MESH = pl.DeviceIdType.MESH
DMA = pltpu.SemaphoreType.DMA


def params(collective):
    return pltpu.CompilerParams(has_side_effects=True, collective_id=collective)


def signal_all(group, cols):
    ep, tp = lax.axis_index('ep'), lax.axis_index('tp')
    barrier = pltpu.get_barrier_semaphore()

    def tell(k, carry):
        peer = {'tp': lax.rem(tp + k // group, cols), 'ep': lax.rem(ep + lax.rem(k, group), group)}
        pl.semaphore_signal(barrier, inc=1, device_id=peer, device_id_type=MESH)
        return carry

    lax.fori_loop(1, group * cols, tell, 0)


def wait_all(group, cols):
    pl.semaphore_wait(pltpu.get_barrier_semaphore(), group * cols - 1)


def post(src, dst, to_ep, to_tp, send_sem, recv_sem):
    ep, tp = lax.axis_index('ep'), lax.axis_index('tp')
    here = jnp.logical_and(to_ep == ep, to_tp == tp)

    @pl.when(jnp.logical_not(here))
    def _():
        pltpu.make_async_remote_copy(src, dst, send_sem, recv_sem, device_id={'tp': to_tp, 'ep': to_ep}, device_id_type=MESH).start()

    @pl.when(here)
    def _():
        pltpu.make_async_copy(src, dst, recv_sem).start()


def await_bytes(ref, sem):
    pltpu.make_async_copy(ref, ref, sem).wait()


def front_kernel(group, cols, send_ref, w_ref, rows_ref, mine_ref, other_ref, rsend, rrecv, wsend, wrecv, osend, orecv):
    ep, tp = lax.axis_index('ep'), lax.axis_index('tp')
    core = lax.rem(ep, 2)
    slots = w_ref.shape[0]
    signal_all(group, cols)
    wait_all(group, cols)

    def weights(k, carry):
        slot = lax.rem(tp + k // 2, slots)
        half = lax.rem(k, 2)
        post(w_ref.at[slot, :, half], mine_ref.at[tp], ep - core + half, slots * core + slot, wsend, wrecv)
        return carry

    lax.fori_loop(0, 2 * slots, weights, 0)

    def rows(k, carry):
        to = lax.rem(ep + k, group)
        post(send_ref.at[to], rows_ref.at[ep], to, tp, rsend, rrecv)
        return carry

    lax.fori_loop(0, group, rows, 0)
    await_bytes(mine_ref, wrecv)
    swap = pltpu.make_async_remote_copy(mine_ref, other_ref, osend, orecv, device_id={'ep': ep + 1 - 2 * core}, device_id_type=MESH)
    swap.start()
    await_bytes(rows_ref, rrecv)
    await_bytes(rows_ref.at[pl.ds(0, group - 1)], rsend)
    own = tp // slots == core

    @pl.when(own)
    def _():
        await_bytes(mine_ref.at[pl.ds(0, 2 * slots - 1)], wsend)

    @pl.when(jnp.logical_not(own))
    def _():
        await_bytes(mine_ref, wsend)

    swap.wait()


def run_front(send, weights, group, cols, collective):
    slots, mats, _, part, width = weights.shape
    piece = jax.ShapeDtypeStruct((cols, mats, part, width), BF16)
    return pl.pallas_call(
        functools.partial(front_kernel, group, cols),
        out_shape=(jax.ShapeDtypeStruct(send.shape, BF16), piece, piece),
        in_specs=[ANY] * 2,
        out_specs=(ANY,) * 3,
        scratch_shapes=[DMA] * 6,
        compiler_params=params(collective),
        cost_estimate=pl.CostEstimate(flops=0, bytes_accessed=120 << 20, transcendentals=0),
    )(send, weights)


def expert_kernel(group, cols, wide, rows_ref, mine_ref, other_ref, dst_ref, out_ref, down_ref, send_sem, recv_sem):
    ep, tp = lax.axis_index('ep'), lax.axis_index('tp')
    me = ep * cols + tp
    width = mine_ref.shape[3]
    half = mine_ref.shape[0] * mine_ref.shape[2]
    feats, n = out_ref.shape[1:]
    pairs = group // 2
    signal_all(group, cols)

    def whole(k):
        return jnp.concatenate([mine_ref[:, k].reshape(half, width), other_ref[:, k].reshape(half, width)], axis=0)

    def plane(i):
        return lax.rem(ep // 2 + 1 + i, pairs)

    def compute(i):
        at = 2 * plane(i)
        rows = jnp.concatenate([rows_ref[at], rows_ref[at + 1]], axis=1 if wide else 0)
        dims = (((1,), (0 if wide else 1,)), ((), ()))
        gate = lax.dot_general(whole(0), rows, dims, preferred_element_type=F32)
        up = lax.dot_general(whole(1), rows, dims, preferred_element_type=F32)
        act = (jax.nn.silu(gate) * up).astype(BF16)
        out = jnp.dot(down_ref[...], act, preferred_element_type=F32).astype(BF16)
        out_ref[pl.ds(at * cols, cols)] = out[:, :n].reshape(cols, feats, n)
        out_ref[pl.ds((at + 1) * cols, cols)] = out[:, n:].reshape(cols, feats, n)

    def send(i):
        at = 2 * plane(i)

        def one(k, carry):
            to_ep = at + lax.rem(k, 2)
            to_tp = lax.rem(tp + k // 2, cols)
            post(out_ref.at[to_ep * cols + to_tp], dst_ref.at[me], to_ep, to_tp, send_sem, recv_sem)
            return carry

        lax.fori_loop(0, 2 * cols, one, 0)

    down_ref[...] = whole(2).T
    compute(0)
    wait_all(group, cols)

    def step(i, carry):
        compute(i)
        send(i - 1)
        return carry

    lax.fori_loop(1, pairs, step, 0)
    send(pairs - 1)
    await_bytes(dst_ref, recv_sem)
    await_bytes(dst_ref.at[pl.ds(0, group * cols - 1)], send_sem)


def run_expert(rows, mine, other, wide, width, half, group, cols, collective):
    ffn = 2 * mine.shape[0] * mine.shape[2]
    blocks = (group * cols, width // cols, half)
    return pl.pallas_call(
        functools.partial(expert_kernel, group, cols, wide),
        out_shape=jax.ShapeDtypeStruct(blocks, BF16),
        in_specs=[VMEM] * 3,
        out_specs=ANY,
        scratch_shapes=[pltpu.VMEM(blocks, BF16), pltpu.VMEM((width, ffn), BF16), DMA, DMA],
        compiler_params=params(collective),
        cost_estimate=pl.CostEstimate(flops=6 * group * half * width * ffn, bytes_accessed=120 << 20, transcendentals=0),
    )(rows, mine, other)


def weigh(cap, cols, first_ref, back_ref, rank_ref, gate_ref, res_ref, acc_ref):
    tokens = rank_ref.shape[1]
    acc_ref[...] = res_ref[...].astype(F32)
    row_iota = lax.broadcasted_iota(jnp.int32, (cap, tokens), 0)

    def step(expert, carry):
        slot = first_ref[expert]
        plane = slot // cols
        block = plane * cols + slot
        rows = jnp.concatenate([back_ref[block], back_ref[block + cols]], axis=1)
        pick = (rank_ref[pl.ds(expert, 1), :] == row_iota).astype(BF16)
        chosen = jnp.dot(rows, pick, preferred_element_type=F32)
        acc_ref[...] += gate_ref[pl.ds(expert, 1), :] * chosen
        return carry

    lax.fori_loop(0, EXPERTS, step, 0)


def middle_kernel(group, cols, cap, first_ref, back_ref, rank_ref, gate_ref, nrank_ref, res_ref, out_ref, dst_ref, send_ref, acc_ref, send_sem, recv_sem):
    ep, tp = lax.axis_index('ep'), lax.axis_index('tp')
    me = ep * cols + tp
    tokens = rank_ref.shape[1]
    half = cap // 2
    all_slots = nrank_ref.shape[0]
    signal_all(group, cols)
    weigh(cap, cols, first_ref, back_ref, rank_ref, gate_ref, res_ref, acc_ref)
    out_ref[...] = acc_ref[...].astype(BF16)
    wait_all(group, cols)
    row_iota = lax.broadcasted_iota(jnp.int32, (cap, tokens), 0)

    def place(i):
        plane = lax.rem(ep // 2 + 1 + lax.rem(i, group // 2), group // 2)
        column = lax.rem(tp + i // (group // 2), cols)
        return plane, column

    def compute(i):
        plane, column = place(i)
        pick = (nrank_ref[pl.ds(plane * cols + column, 1), :] == row_iota).astype(BF16)
        rows = lax.dot_general(out_ref[...], pick, (((1,), (1,)), ((), ())), preferred_element_type=F32).astype(BF16)
        block = 2 * plane * cols + column
        send_ref[block] = rows[:, :half]
        send_ref[block + cols] = rows[:, half:]

    def send(i):
        plane, column = place(i)
        block = 2 * plane * cols + column
        post(send_ref.at[block], dst_ref.at[me], 2 * plane, column, send_sem, recv_sem)
        post(send_ref.at[block + cols], dst_ref.at[me], 2 * plane + 1, column, send_sem, recv_sem)

    compute(0)

    def step(i, carry):
        compute(i)
        send(i - 1)
        return carry

    lax.fori_loop(1, all_slots, step, 0)
    send(all_slots - 1)
    await_bytes(dst_ref, recv_sem)
    await_bytes(dst_ref.at[pl.ds(0, group * cols - 1)], send_sem)


def run_middle(first, back, rank, gate, nrank, residual, group, cols, cap, collective):
    feats, tokens = residual.shape
    return pl.pallas_call(
        functools.partial(middle_kernel, group, cols, cap),
        out_shape=(jax.ShapeDtypeStruct((feats, tokens), BF16), jax.ShapeDtypeStruct(back.shape, BF16)),
        in_specs=[SMEM] + [VMEM] * 5,
        out_specs=(VMEM, ANY),
        scratch_shapes=[pltpu.VMEM(back.shape, BF16), pltpu.VMEM((feats, tokens), F32), DMA, DMA],
        compiler_params=params(collective),
        cost_estimate=pl.CostEstimate(flops=2 * EXPERTS * cap * 256 * tokens, bytes_accessed=120 << 20, transcendentals=0),
    )(first, back, rank, gate, nrank, residual)


def last_kernel(group, cols, side, cap, first_ref, back_ref, rank_ref, gate_ref, res_ref, dst_ref, out_ref, acc_ref, own_sem, send_sem, recv_sem):
    ep, tp = lax.axis_index('ep'), lax.axis_index('tp')
    z, y = tp // side, lax.rem(tp, side)
    feats = out_ref.shape[0]
    cut = feats // 2
    low, high = pl.ds(0, cut), pl.ds(cut, cut)
    signal_all(group, cols)
    weigh(cap, cols, first_ref, back_ref, rank_ref, gate_ref, res_ref, acc_ref)
    out_ref[...] = acc_ref[...].astype(BF16)
    own = pltpu.make_async_copy(out_ref, dst_ref.at[z, y], own_sem)
    own.start()
    own.wait()
    wait_all(group, cols)

    def push(ref, to_z, to_y, k):
        pltpu.make_async_remote_copy(ref, ref, send_sem.at[k], recv_sem.at[k], device_id={'tp': to_z * side + to_y}, device_id_type=MESH).start()

    for j in range(1, side):
        push(dst_ref.at[z, y, low], z, lax.rem(y + j, side), 0)
        push(dst_ref.at[z, y, high], lax.rem(z + j, side), y, 1)
    some = pl.ds(0, side - 1)
    await_bytes(dst_ref.at[z, some, low], recv_sem.at[0])
    for j in range(1, side):
        push(dst_ref.at[z, :, low], lax.rem(z + j, side), y, 2)
    await_bytes(dst_ref.at[some, y, high], recv_sem.at[1])
    for j in range(1, side):
        push(dst_ref.at[:, y, high], z, lax.rem(y + j, side), 3)
    await_bytes(dst_ref.at[some, :, low], recv_sem.at[2])
    await_bytes(dst_ref.at[:, some, high], recv_sem.at[3])
    await_bytes(dst_ref.at[z, some, low], send_sem.at[0])
    await_bytes(dst_ref.at[some, y, high], send_sem.at[1])
    await_bytes(dst_ref.at[some, :, low], send_sem.at[2])
    await_bytes(dst_ref.at[:, some, high], send_sem.at[3])


def run_last(first, back, rank, gate, residual, group, cols, cap, collective):
    feats, tokens = residual.shape
    side = int(round(cols ** 0.5))
    return pl.pallas_call(
        functools.partial(last_kernel, group, cols, side, cap),
        out_shape=jax.ShapeDtypeStruct((side, side, feats, tokens), BF16),
        in_specs=[SMEM] + [VMEM] * 4,
        out_specs=ANY,
        scratch_shapes=[pltpu.VMEM((feats, tokens), BF16), pltpu.VMEM((feats, tokens), F32), DMA, DMA((4,)), DMA((4,))],
        compiler_params=params(collective),
        cost_estimate=pl.CostEstimate(flops=2 * EXPERTS * cap * 256 * tokens, bytes_accessed=120 << 20, transcendentals=0),
    )(first, back, rank, gate, residual)


def solution(mesh):
    group = mesh.shape['ep']
    cols = mesh.shape['tp']
    row_spec = P(('rep', 'ep'), None)
    layer_spec = P(None, ('rep', 'ep'), None)
    col_spec = P(None, ('rep', 'ep'), None, 'tp')
    down_spec = P(None, ('rep', 'ep'), 'tp', None)
    map_spec = P(None, None)

    def device_step(x_in, route_ids, gate_vals, w_gate, w_up, w_down, old_map, move_src, move_dst):
        layers, slots, width, part = w_gate.shape
        tokens, top_k = route_ids.shape[1], route_ids.shape[2]
        all_slots = group * slots
        cap = 2 * tokens * top_k // all_slots
        half = cap // 2
        feats = width // cols
        ep = lax.axis_index('ep')
        tp = lax.axis_index('tp')
        core = ep % 2
        partner = [(i, i ^ 1) for i in range(group)]
        packed = jnp.stack([jnp.swapaxes(w_gate, 2, 3), jnp.swapaxes(w_up, 2, 3), w_down], axis=2)

        tables = []
        expert_ids = jnp.arange(EXPERTS, dtype=jnp.int32)
        slot_ids = jnp.arange(all_slots, dtype=jnp.int32)
        before = (jnp.arange(tokens)[:, None] < jnp.arange(tokens)[None, :]).astype(BF16)
        for layer in range(layers):
            ids = route_ids[layer].T
            match = ids[None, :, :] == expert_ids[:, None, None]
            taken = jnp.any(match, axis=1)
            gate = jnp.sum(jnp.where(match, gate_vals[layer].T[None], 0.0), axis=1)
            rank = jnp.dot(taken.astype(BF16), before, preferred_element_type=F32).astype(jnp.int32)
            rank = jnp.where(taken, rank, -1)
            holds = old_map[layer][None, :] == expert_ids[:, None]
            first = jnp.min(jnp.where(holds, slot_ids[None, :], all_slots - 1), axis=1)
            tables.append((rank, gate, first))

        rank, gate, first = tables[0]
        my_slots = jnp.arange(group // 2, dtype=jnp.int32) * cols + tp
        serves = first[:, None] == my_slots[None, :]
        picked = jnp.sum(jnp.where(serves[:, :, None], rank[:, None, :] + 1, 0), axis=0) - 1
        row = jnp.arange(cap, dtype=jnp.int32)
        pick = (picked[:, None, :] == row[None, :, None]).astype(BF16).reshape(group * half, tokens)
        send = jnp.dot(pick, x_in, preferred_element_type=F32).astype(BF16).reshape(group, half, width)
        cut = packed.reshape(layers, slots, 3, 2, part // 2, width)
        rows, mine, other = run_front(send, cut[0], group, cols, 0)
        rows, later = lax.optimization_barrier((rows, packed))

        cut1 = later.reshape(layers, slots, 3, 2, part // 2, width)[1]
        keep = lax.dynamic_index_in_dim(cut1, core, 2, keepdims=False)
        give = lax.dynamic_index_in_dim(cut1, 1 - core, 2, keepdims=False)
        take = lax.ppermute(give, 'ep', partner)
        wsend = jnp.where(core == 0, jnp.stack([keep, take]), jnp.stack([take, keep])).reshape(2 * slots, 3, part // 2, width)
        mine1 = lax.all_to_all(wsend, 'tp', 0, 0, tiled=True)
        residual = lax.dynamic_slice_in_dim(x_in, tp * feats, feats, axis=1).T
        nrank, ngate, nfirst = tables[1]
        serving = (nfirst[:, None] == slot_ids[None, :])
        by_slot = jnp.sum(jnp.where(serving[:, :, None], nrank[:, None, :] + 1, 0), axis=0) - 1
        back = run_expert(rows, mine, other, False, width, half, group, cols, 1)
        back, mine1, later = lax.optimization_barrier((back, mine1, later))
        other1 = lax.ppermute(mine1, 'ep', partner)

        pieces = group // layers
        depth = 3 * part // pieces
        cut2 = later.reshape(layers, slots, pieces, depth, width).transpose(0, 2, 1, 3, 4).reshape(group, slots, depth, width)
        held = lax.all_to_all(cut2, 'ep', 0, 0, tiled=True).reshape(all_slots, depth, width)

        residual, rows = run_middle(first, back, rank, gate, by_slot, residual, group, cols, cap, 2)
        rows, other1, held = lax.optimization_barrier((rows, other1, held))
        source = jnp.arange(all_slots, dtype=jnp.int32)
        my_layer = ep // pieces
        source = source.at[move_dst[my_layer]].set(move_src[my_layer])
        got = lax.all_to_all(held[source].reshape(group, slots, depth, width), 'ep', 0, 0, tiled=True)

        rows = rows.reshape(group, width, half)
        back = run_expert(rows, mine1, other1, True, width, half, group, cols, 3)
        y_out = run_last(nfirst, back, nrank, ngate, residual, group, cols, cap, 4).reshape(width, tokens).T

        new = got.reshape(layers, pieces, slots, depth, width).transpose(0, 2, 1, 3, 4).reshape(layers, slots, 3, part, width)
        return y_out, jnp.swapaxes(new[:, :, 0], 2, 3), jnp.swapaxes(new[:, :, 1], 2, 3), new[:, :, 2]

    return jax.shard_map(device_step, mesh=mesh, in_specs=(row_spec, layer_spec, layer_spec, col_spec, col_spec, down_spec, map_spec, map_spec, map_spec), out_specs=(row_spec, col_spec, col_spec, down_spec), check_vma=False)
```

time: 654 us -> 430 us (0.66)
  Pallas kernels: 27.4 us -> 353 us
  waiting for transfers between devices: 313 us -> 2.8 us
  blocking collectives: 142 us -> 0 us
  matrix products: 40 us -> 7.74 us
  starting transfers between devices: 46.2 us -> 16.5 us
  local copies, waits for them, and re-layouts: 60.6 us -> 35 us
  between operations: 14.4 us -> 0.9 us
    pallas_call x2 -> x5, Pallas kernels: 27.4 us -> 353 us  [the longest x2 175 us: run_expert(): pl.pallas_call(functools.partial(expert_kernel, group, cols, wide), out_s...]
    all_to_all x7 -> x3, waiting for transfers between devices: 228 us -> 0.01 us  [the longest x1 0.01 us: device_step(): lax.all_to_all(held[source].reshape(group, slots, depth, width), 'ep', 0,...]
    all_to_all x3 -> x0, blocking collectives: 142 us -> none  [the longest x2 82.9 us: device_step(): lax.all_to_all(out.reshape(group, half, width), 'ep', 0, 0, tiled=True)]
    all_gather x2 -> x0, waiting for transfers between devices: 85.3 us -> none  [device_step(): hidden = lax.all_gather(residual, 'tp', axis=0, tiled=True)]
    dot_general x6 -> x1, matrix products: 37.9 us -> 4.75 us  [device_step(): jnp.dot(pick, x_in, preferred_element_type=F32).astype(BF16)]
    all_to_all x7 -> x3, starting transfers between devices: 46 us -> 16.2 us  [the longest x1 6.38 us: device_step(): mine1 = lax.all_to_all(wsend, 'tp', 0, 0, tiled=True)]
    all_to_all x2 -> x0, local copies, waits for them, and re-layouts: 10.8 us -> none  [device_step(): back = lax.all_to_all(back, 'tp', 0, 0, tiled=True)]
  transfers between devices with their start and end apart: 9 -> 5, of which waited for: 7 -> 1; matrix products, arithmetic and copies ran while one was open for 8% -> 3% of each run, Pallas kernels for 2% -> 71%
where the time goes in v3:
time: 430 us; the launch traced here: 429 us
  Pallas kernels  353 us (82%)
  local copies, waits for them, and re-layouts  35 us (8%)
  starting transfers between devices  16.5 us (4%)
  other arithmetic  13 us (3%)
  matrix products  7.74 us (2%)
    pallas_call x2, Pallas kernels, run_expert(): pl.pallas_call(functools.partial(expert_kernel, group, cols, wide), out_s...  175 us
    pallas_call x1, Pallas kernels, run_middle(): pl.pallas_call(functools.partial(middle_kernel, group, cols, cap), out_sh...  90 us
    pallas_call x1, Pallas kernels, run_front(): pl.pallas_call(functools.partial(front_kernel, group, cols), out_shape=(j...  46.7 us
    pallas_call x1, Pallas kernels, run_last(): pl.pallas_call(functools.partial(last_kernel, group, cols, side, cap), ou...  41.5 us
  transfers between devices with their start and end apart: 5, of which 1 were waited for; matrix products, arithmetic and copies ran while one was open for 3% of the time, Pallas kernels for 71%

profile of v3, /device:TPU:1, one launch (start us, length us, event | category | flops | bytes accessed | tf_op | source)
XLA Modules:
  0.0 429.0 jit_solution(3560866143854911832)
XLA Ops:
  0.6 0.0 copy-start
  0.7 0.9 slice_bitcast_fusion.7
  1.5 0.9 slice_bitcast_fusion.4
  2.4 1.6 fusion.2
  4.0 1.1 broadcast_add_fusion.2
  5.0 0.1 select_reduce_fusion.4
  5.1 0.0 copy-start.5
  5.1 0.0 copy-start.4
  5.2 0.1 broadcast_compare_fusion
  5.2 0.1 select_reduce_fusion.3
  5.4 2.6 pad_maximum_fusion
  8.0 0.0 copy-done.5
  8.0 0.0 copy-start.2
  8.0 1.7 slice.48
  9.7 1.2 copy-done.2
  10.9 0.7 bitcast_compare_fusion
  11.6 0.0 copy-done
  11.6 4.8 %convolution_convert_fusion = bf16[1024,1536]{1,0:T(8,128)(2,1)} fusion(pred[1024,1024]{1,0:T(32,128)(4,1)S(1)} %bitcast_compare_fusion, bf16[1024,1536]{1,0:T(8,128)(2,1)S(1)} %copy-done), kind=kOutput, calls=%fused_computation.8 | convolution fusion | flops 3222798336 | bytes 7340032 | tf_op jit(solution)/shard_map/dot_general | solution.py:343
  16.3 46.7 %shard_map.120 = (bf16[8,128,1536]{2,1,0:T(8,128)(2,1)}, bf16[16,3,16,1536]{3,2,1,0:T(8,128)(2,1)}, bf16[16,3,16,1536]{3,2,1,0:T(8,128)(2,1)}) custom-call(bf16[8,128,1536]{2,1,0:T(8,128)(2,1)} %bitcast.88, bf16[8,3,2,16,1536]{4,3,2,1,0:T(8,128)(2,1)} %bitcast.85), custom_call_target="tpu_custom_call" | custom-call | bytes 125829120 | tf_op jit(solution)/shard_map/pallas_call | solution.py:99
  63.1 3.3 slice.39
  66.4 3.2 dynamic-slice_bitcast_fusion.1
  69.6 0.0 collective-permute-start
  69.6 2.8 collective-permute-done
  72.4 4.4 %maximum_select_fusion = bf16[2,8,3,16,1536]{4,3,2,1,0:T(8,128)(2,1)} fusion(bf16[1,8,3,16,1536]{4,3,2,1,0:T(8,128)(2,1)} %bitcast.15, bf16[1,8,3,16,1536]{4,3,2,1,0:T(8,128)(2,1)} %get-tuple-element.33, pred[]{:T(512)S(6)} %eq.133), kind=kLoop, calls=%fused_computation.9 | loop fusion | flops 3538944 | bytes 4718593 | tf_op jit(solution)/shard_map/jit(_where)/select_n | solution.py:352
  76.8 6.4 %all-to-all-start = ((bf16[16,3,16,1536]{3,2,1,0:T(8,128)(2,1)}), bf16[16,3,16,1536]{3,2,1,0:T(8,128)(2,1)}, u32[]{:S(2)}, u32[]{:S(2)}) async-start(bf16[16,3,16,1536]{3,2,1,0:T(8,128)(2,1)} %bitcast.84), calls=%async_computation | async-start | bytes 4718592 | tf_op jit(solution)/shard_map/all_to_all | solution.py:353
  83.2 73.2 %shard_map.121.back_ref = bf16[128,96,128]{2,1,0:T(8,128)(2,1)} custom-call(bf16[8,128,1536]{2,1,0:T(8,128)(2,1)} %get-tuple-element.18.rows_ref, bf16[16,3,16,1536]{3,2,1,0:T(8,128)(2,1)} %get-tuple-element.19.mine_ref, bf16[16,3,16,1536]{3,2,1,0:T(8,128)(2,1)} %get-tuple-element.20.other_ref), custom_call_target="tpu_custom_call" | custom-call | flops 4831838208 | bytes 125829120 | tf_op jit(solution)/shard_map/pallas_call | solution.py:165
  156.4 0.0 all-to-all-done.mine_ref
  156.4 4.9 %copy.26 = bf16[2,4,8,24,1536]{4,3,2,1,0:T(8,128)(2,1)} copy(bf16[2,4,8,24,1536]{4,3,1,2,0:T(8,128)(2,1)} %bitcast.79) | data formatting | bytes 9437184 | tf_op jit(solution)/shard_map/transpose | solution.py:364
  161.4 0.0 copy-start.7
  161.4 0.0 copy-start.8
  161.4 0.0 copy-start.3
  161.4 4.9 %all-to-all-start.1 = ((bf16[8,8,24,1536]{3,2,1,0:T(8,128)(2,1)}), bf16[8,8,24,1536]{3,2,1,0:T(8,128)(2,1)}, u32[]{:S(2)}, u32[]{:S(2)}) async-start(bf16[8,8,24,1536]{3,2,1,0:T(8,128)(2,1)} %bitcast.80), calls=%async_computation.1 | async-start | bytes 9437184 | tf_op jit(solution)/shard_map/all_to_all | solution.py:365
  166.3 0.1 constant_dynamic-slice_fusion.1
  166.4 0.2 collective-permute-start.1
  166.7 0.0 copy-done.7
  166.7 0.8 copy.29
  167.5 0.0 copy-done.8
  167.5 0.7 scatter_fusion
  168.2 0.0 copy-done.3
  168.2 1.5 select_reduce_fusion.1
  169.8 0.0 copy-done.4
  169.8 0.1 iota_compare_fusion.13
  169.8 1.9 broadcast_add_fusion.1
  171.8 1.0 select_reduce_fusion
  172.8 0.7 broadcast_add_fusion.nrank_ref
  173.5 90.0 %shard_map.122 = (bf16[96,1024]{1,0:T(8,128)(2,1)}, bf16[128,96,128]{2,1,0:T(8,128)(2,1)}) custom-call(s32[40]{0:T(128)} %copy-done.5, bf16[128,96,128]{2,1,0:T(8,128)(2,1)} %shard_map.121.back_ref, s32[40,1024]{1,0:T(8,128)} %get-tuple-element.42.rank_ref, f32[40,1024]{1,0:T(8,128)} %get-tuple-element.48.gate_ref, s32[64,1024]{1,0:T(8,128)} %broadcast_add_fusion.nrank_ref, ...), custom_call_target="tpu_custom_call" | custom-call | flops 5368709120 | bytes 125829120 | tf_op jit(solution)/shard_map/pallas_call | solution.py:240
  263.5 0.0 collective-permute-done.1.other_ref
  263.6 0.0 copy-start.6
  263.6 0.0 all-to-all-done.1
  263.6 6.2 %gather_fusion = bf16[64,24,1536]{2,1,0:T(8,128)(2,1)} fusion(bf16[64,24,1536]{2,1,0:T(8,128)(2,1)} %bitcast.25, s32[1024]{0:T(1024)S(1)} %pad_clamp_fusion), kind=kCustom, calls=%fused_computation | custom fusion | bytes 9437440 | tf_op jit(solution)/shard_map/gather | solution.py:372
  269.8 0.0 copy-done.6
  269.8 5.0 %all-to-all-start.2 = ((bf16[8,8,24,1536]{3,2,1,0:T(8,128)(2,1)}), bf16[8,8,24,1536]{3,2,1,0:T(8,128)(2,1)}, u32[]{:S(2)}, u32[]{:S(2)}) async-start(bf16[8,8,24,1536]{3,2,1,0:T(8,128)(2,1)} %bitcast.81), calls=%async_computation.2 | async-start | bytes 9437184 | tf_op jit(solution)/shard_map/all_to_all | solution.py:372
  274.7 101.6 %shard_map.123.back_ref = bf16[128,96,128]{2,1,0:T(8,128)(2,1)} custom-call(bf16[8,1536,128]{2,1,0:T(8,128)(2,1)} %bitcast.94, bf16[16,3,16,1536]{3,2,1,0:T(8,128)(2,1)} %all-to-all-done.mine_ref, bf16[16,3,16,1536]{3,2,1,0:T(8,128)(2,1)} %copy-done.6), custom_call_target="tpu_custom_call" | custom-call | flops 4831838208 | bytes 125829120 | tf_op jit(solution)/shard_map/pallas_call | solution.py:165
  376.4 41.5 %shard_map.124 = bf16[4,4,96,1024]{3,2,1,0:T(8,128)(2,1)} custom-call(s32[40]{0:T(128)} %copy-done.4, bf16[128,96,128]{2,1,0:T(8,128)(2,1)} %shard_map.123.back_ref, s32[40,1024]{1,0:T(8,128)} %get-tuple-element.44.rank_ref, f32[40,1024]{1,0:T(8,128)} %get-tuple-element.47.gate_ref, bf16[96,1024]{1,0:T(8,128)(2,1)} %get-tuple-element.28.res_ref), custom_call_target="tpu_custom_call" | custom-call | flops 5368709120 | bytes 125829120 | tf_op jit(solution)/shard_map/pallas_call | solution.py:289
  417.9 4.6 %copy.27 = bf16[1536,1024]{0,1:T(8,128)(2,1)} copy(bf16[1536,1024]{1,0:T(8,128)(2,1)} %bitcast.87) | data formatting | bytes 6291456 | tf_op jit(solution)/shard_map/reshape | solution.py:376
  422.6 0.0 all-to-all-done.2
  422.6 2.8 copy.28
  425.4 0.0 copy-start.1
  425.4 2.5 slice_bitcast_fusion
  427.9 1.1 copy-done.1
  (10 shorter events, 0.0 us)
Async XLA Ops:
  0.6 11.0 %copy-start = (bf16[1024,1536]{1,0:T(8,128)(2,1)S(1)}, bf16[1024,1536]{1,0:T(8,128)(2,1)}, u32[]{:S(2)}) copy-start(bf16[1024,1536]{1,0:T(8,128)(2,1)} %param.9) | copy-start | bytes 9437188
  5.1 2.9 copy-start.5
  5.1 164.6 %copy-start.4 = (s32[40]{0:T(128)}, s32[40]{0:T(128)S(1)}, u32[]{:S(2)}) copy-start(s32[40]{0:T(128)S(1)} %get-tuple-element.46.first_ref) | copy-start | bytes 484
  8.0 2.9 copy-start.2
  69.6 2.8 collective-permute-start
  76.8 79.6 %all-to-all-start = ((bf16[16,3,16,1536]{3,2,1,0:T(8,128)(2,1)}), bf16[16,3,16,1536]{3,2,1,0:T(8,128)(2,1)}, u32[]{:S(2)}, u32[]{:S(2)}) async-start(bf16[16,3,16,1536]{3,2,1,0:T(8,128)(2,1)} %bitcast.84), calls=%async_computation | async-start | bytes 4718592 | tf_op jit(solution)/shard_map/all_to_all | solution.py:353
  161.4 5.3 %copy-start.7 = (s32[2,32]{1,0:T(2,128)S(1)}, s32[2,32]{1,0:T(2,128)}, u32[]{:S(2)}) copy-start(s32[2,32]{1,0:T(2,128)} %param.17) | copy-start | bytes 772
  161.4 6.1 %copy-start.8 = (s32[2,32]{1,0:T(2,128)S(1)}, s32[2,32]{1,0:T(2,128)}, u32[]{:S(2)}) copy-start(s32[2,32]{1,0:T(2,128)} %param.16) | copy-start | bytes 772
  161.4 6.9 %copy-start.3 = (f32[2,1024,8]{1,2,0:T(8,128)S(1)}, f32[2,1024,8]{1,2,0:T(8,128)}, u32[]{:S(2)}) copy-start(f32[2,1024,8]{1,2,0:T(8,128)} %param.11) | copy-start | bytes 196612
  161.4 102.2 %all-to-all-start.1 = ((bf16[8,8,24,1536]{3,2,1,0:T(8,128)(2,1)}), bf16[8,8,24,1536]{3,2,1,0:T(8,128)(2,1)}, u32[]{:S(2)}, u32[]{:S(2)}) async-start(bf16[8,8,24,1536]{3,2,1,0:T(8,128)(2,1)} %bitcast.80), calls=%async_computation.1 | async-start | bytes 9437184 | tf_op jit(solution)/shard_map/all_to_all | solution.py:365
  166.4 97.1 %collective-permute-start.1 = (bf16[16,3,16,1536]{3,2,1,0:T(8,128)(2,1)}, bf16[16,3,16,1536]{3,2,1,0:T(8,128)(2,1)S(1)}, u32[]{:S(2)}, u32[]{:S(2)}) collective-permute-start(bf16[16,3,16,1536]{3,2,1,0:T(8,128)(2,1)} %all-to-all-done.mine_ref), channel_id=1, source_target_pairs={{0,1},{1,0},{2,3},{3,2},{4,5},{5,4},{6,7},{7,6},{8,9},{9,8},{10,11... | collective-permute-start | bytes 7077896 | tf_op jit(solution)/shard_map/ppermute | solution.py:360
  263.6 6.2 %copy-start.6 = (bf16[16,3,16,1536]{3,2,1,0:T(8,128)(2,1)}, bf16[16,3,16,1536]{3,2,1,0:T(8,128)(2,1)S(1)}, u32[]{:S(2)}) copy-start(bf16[16,3,16,1536]{3,2,1,0:T(8,128)(2,1)S(1)} %collective-permute-done.1.other_ref) | copy-start | bytes 7077892
  269.8 152.8 %all-to-all-start.2 = ((bf16[8,8,24,1536]{3,2,1,0:T(8,128)(2,1)}), bf16[8,8,24,1536]{3,2,1,0:T(8,128)(2,1)}, u32[]{:S(2)}, u32[]{:S(2)}) async-start(bf16[8,8,24,1536]{3,2,1,0:T(8,128)(2,1)} %bitcast.81), calls=%async_computation.2 | async-start | bytes 9437184 | tf_op jit(solution)/shard_map/all_to_all | solution.py:372
  425.4 3.6 copy-start.1

commit v4 on v3

--- a/solution.py
+++ b/solution.py
@@ -54,57 +54,77 @@
     pltpu.make_async_copy(ref, ref, sem).wait()
 
 
-def front_kernel(group, cols, send_ref, w_ref, rows_ref, mine_ref, other_ref, rsend, rrecv, wsend, wrecv, osend, orecv):
+def front_kernel(group, cols, cap, x_ref, picked_ref, g_ref, u_ref, d_ref, rows_ref, mine0_ref, other0_ref, mine1_ref, other1_ref, send_ref, rsend, rrecv, wsend, wrecv, osend, orecv):
     ep, tp = lax.axis_index('ep'), lax.axis_index('tp')
     core = lax.rem(ep, 2)
-    slots = w_ref.shape[0]
+    slots = g_ref.shape[1]
+    half = cap // 2
+    mines, others = (mine0_ref, mine1_ref), (other0_ref, other1_ref)
     signal_all(group, cols)
+    row_iota = lax.broadcasted_iota(jnp.int32, (cap, x_ref.shape[0]), 0)
+
+    def compute(i, carry):
+        pick = (picked_ref[pl.ds(i, 1), :] == row_iota).astype(BF16)
+        rows = jnp.dot(pick, x_ref[...], preferred_element_type=F32).astype(BF16)
+        send_ref[2 * i] = rows[:half]
+        send_ref[2 * i + 1] = rows[half:]
+        return carry
+
+    lax.fori_loop(0, group // 2, compute, 0)
     wait_all(group, cols)
 
-    def weights(k, carry):
-        slot = lax.rem(tp + k // 2, slots)
-        half = lax.rem(k, 2)
-        post(w_ref.at[slot, :, half], mine_ref.at[tp], ep - core + half, slots * core + slot, wsend, wrecv)
-        return carry
-
-    lax.fori_loop(0, 2 * slots, weights, 0)
+    def weights(layer):
+        def one(k, carry):
+            slot = lax.rem(tp + k // 2, slots)
+            part = lax.rem(k, 2)
+            for mat, ref in enumerate((g_ref, u_ref, d_ref)):
+                post(ref.at[layer, slot, part], mines[layer].at[tp, mat], ep - core + part, slots * core + slot, wsend.at[layer], wrecv.at[layer])
+            return carry
+
+        lax.fori_loop(0, 2 * slots, one, 0)
 
     def rows(k, carry):
         to = lax.rem(ep + k, group)
         post(send_ref.at[to], rows_ref.at[ep], to, tp, rsend, rrecv)
         return carry
 
+    weights(0)
     lax.fori_loop(0, group, rows, 0)
-    await_bytes(mine_ref, wrecv)
-    swap = pltpu.make_async_remote_copy(mine_ref, other_ref, osend, orecv, device_id={'ep': ep + 1 - 2 * core}, device_id_type=MESH)
-    swap.start()
+    weights(1)
+    swaps = []
+    for layer in range(2):
+        await_bytes(mines[layer], wrecv.at[layer])
+        swap = pltpu.make_async_remote_copy(mines[layer], others[layer], osend.at[layer], orecv.at[layer], device_id={'ep': ep + 1 - 2 * core}, device_id_type=MESH)
+        swap.start()
+        swaps.append(swap)
     await_bytes(rows_ref, rrecv)
     await_bytes(rows_ref.at[pl.ds(0, group - 1)], rsend)
     own = tp // slots == core
-
-    @pl.when(own)
-    def _():
-        await_bytes(mine_ref.at[pl.ds(0, 2 * slots - 1)], wsend)
-
-    @pl.when(jnp.logical_not(own))
-    def _():
-        await_bytes(mine_ref, wsend)
-
-    swap.wait()
-
-
-def run_front(send, weights, group, cols, collective):
-    slots, mats, _, part, width = weights.shape
-    piece = jax.ShapeDtypeStruct((cols, mats, part, width), BF16)
+    for layer in range(2):
+        @pl.when(own)
+        def _():
+            await_bytes(mines[layer].at[pl.ds(0, 2 * slots - 1)], wsend.at[layer])
+
+        @pl.when(jnp.logical_not(own))
+        def _():
+            await_bytes(mines[layer], wsend.at[layer])
+
+        swaps[layer].wait()
+
+
+def run_front(x, picked, gates, ups, downs, group, cols, cap, collective):
+    _, slots, _, part, width = gates.shape
+    piece = jax.ShapeDtypeStruct((cols, 3, part, width), BF16)
+    rows = (group, cap // 2, width)
     return pl.pallas_call(
-        functools.partial(front_kernel, group, cols),
-        out_shape=(jax.ShapeDtypeStruct(send.shape, BF16), piece, piece),
-        in_specs=[ANY] * 2,
-        out_specs=(ANY,) * 3,
-        scratch_shapes=[DMA] * 6,
+        functools.partial(front_kernel, group, cols, cap),
+        out_shape=(jax.ShapeDtypeStruct(rows, BF16),) + (piece,) * 4,
+        in_specs=[VMEM] * 2 + [ANY] * 3,
+        out_specs=(ANY,) * 5,
+        scratch_shapes=[pltpu.VMEM(rows, BF16), DMA, DMA] + [DMA((2,))] * 4,
         compiler_params=params(collective),
-        cost_estimate=pl.CostEstimate(flops=0, bytes_accessed=120 << 20, transcendentals=0),
-    )(send, weights)
+        cost_estimate=pl.CostEstimate(flops=0, bytes_accessed=240 << 20, transcendentals=0),
+    )(x, picked, gates, ups, downs)
 
 
 def expert_kernel(group, cols, wide, rows_ref, mine_ref, other_ref, dst_ref, out_ref, down_ref, send_sem, recv_sem):
@@ -315,9 +335,6 @@
         feats = width // cols
         ep = lax.axis_index('ep')
         tp = lax.axis_index('tp')
-        core = ep % 2
-        partner = [(i, i ^ 1) for i in range(group)]
-        packed = jnp.stack([jnp.swapaxes(w_gate, 2, 3), jnp.swapaxes(w_up, 2, 3), w_down], axis=2)
 
         tables = []
         expert_ids = jnp.arange(EXPERTS, dtype=jnp.int32)
@@ -338,41 +355,31 @@
         my_slots = jnp.arange(group // 2, dtype=jnp.int32) * cols + tp
         serves = first[:, None] == my_slots[None, :]
         picked = jnp.sum(jnp.where(serves[:, :, None], rank[:, None, :] + 1, 0), axis=0) - 1
-        row = jnp.arange(cap, dtype=jnp.int32)
-        pick = (picked[:, None, :] == row[None, :, None]).astype(BF16).reshape(group * half, tokens)
-        send = jnp.dot(pick, x_in, preferred_element_type=F32).astype(BF16).reshape(group, half, width)
-        cut = packed.reshape(layers, slots, 3, 2, part // 2, width)
-        rows, mine, other = run_front(send, cut[0], group, cols, 0)
-        rows, later = lax.optimization_barrier((rows, packed))
-
-        cut1 = later.reshape(layers, slots, 3, 2, part // 2, width)[1]
-        keep = lax.dynamic_index_in_dim(cut1, core, 2, keepdims=False)
-        give = lax.dynamic_index_in_dim(cut1, 1 - core, 2, keepdims=False)
-        take = lax.ppermute(give, 'ep', partner)
-        wsend = jnp.where(core == 0, jnp.stack([keep, take]), jnp.stack([take, keep])).reshape(2 * slots, 3, part // 2, width)
-        mine1 = lax.all_to_all(wsend, 'tp', 0, 0, tiled=True)
+        cut = (layers, slots, 2, part // 2, width)
+        w_g, w_u = jnp.swapaxes(w_gate, 2, 3), jnp.swapaxes(w_up, 2, 3)
+        rows, mine, other, mine1, other1 = run_front(x_in, picked, w_g.reshape(cut), w_u.reshape(cut), w_down.reshape(cut), group, cols, cap, 0)
+
+        pieces = group // layers
+        depth = 3 * part // pieces
+        packed = jnp.stack([w_g, w_u, w_down], axis=2)
+        cut2 = packed.reshape(layers, slots, pieces, depth, width).transpose(0, 2, 1, 3, 4).reshape(group, slots, depth, width)
+        held = lax.all_to_all(cut2, 'ep', 0, 0, tiled=True).reshape(all_slots, depth, width)
+        rows, mine, held = lax.optimization_barrier((rows, mine, held))
+        source = jnp.arange(all_slots, dtype=jnp.int32)
+        my_layer = ep // pieces
+        source = source.at[move_dst[my_layer]].set(move_src[my_layer])
+        held = held[source].reshape(group, slots, depth, width)
+
         residual = lax.dynamic_slice_in_dim(x_in, tp * feats, feats, axis=1).T
         nrank, ngate, nfirst = tables[1]
         serving = (nfirst[:, None] == slot_ids[None, :])
         by_slot = jnp.sum(jnp.where(serving[:, :, None], nrank[:, None, :] + 1, 0), axis=0) - 1
         back = run_expert(rows, mine, other, False, width, half, group, cols, 1)
-        back, mine1, later = lax.optimization_barrier((back, mine1, later))
-        other1 = lax.ppermute(mine1, 'ep', partner)
-
-        pieces = group // layers
-        depth = 3 * part // pieces
-        cut2 = later.reshape(layers, slots, pieces, depth, width).transpose(0, 2, 1, 3, 4).reshape(group, slots, depth, width)
-        held = lax.all_to_all(cut2, 'ep', 0, 0, tiled=True).reshape(all_slots, depth, width)
-
         residual, rows = run_middle(first, back, rank, gate, by_slot, residual, group, cols, cap, 2)
-        rows, other1, held = lax.optimization_barrier((rows, other1, held))
-        source = jnp.arange(all_slots, dtype=jnp.int32)
-        my_layer = ep // pieces
-        source = source.at[move_dst[my_layer]].set(move_src[my_layer])
-        got = lax.all_to_all(held[source].reshape(group, slots, depth, width), 'ep', 0, 0, tiled=True)
-
         rows = rows.reshape(group, width, half)
         back = run_expert(rows, mine1, other1, True, width, half, group, cols, 3)
+        back, held = lax.optimization_barrier((back, held))
+        got = lax.all_to_all(held, 'ep', 0, 0, tiled=True)
         y_out = run_last(nfirst, back, nrank, ngate, residual, group, cols, cap, 4).reshape(width, tokens).T
 
         new = got.reshape(layers, pieces, slots, depth, width).transpose(0, 2, 1, 3, 4).reshape(layers, slots, 3, part, width)

time: 430 us -> 371 us (0.86)
  Pallas kernels: 353 us -> 322 us
  local copies, waits for them, and re-layouts: 35 us -> 20.3 us
  starting transfers between devices: 16.5 us -> 10.6 us
  matrix products: 7.74 us -> 2.14 us
  other arithmetic: 13 us -> 7.89 us
    pallas_call x2, Pallas kernels: 175 us -> 129 us  [run_expert(): pl.pallas_call(functools.partial(expert_kernel, group, cols, wide), out_s...]
    pallas_call x1, Pallas kernels: 46.7 us -> 82.7 us  [run_front(): pl.pallas_call(functools.partial(front_kernel, group, cols, cap), out_sha...]
    pallas_call x1, Pallas kernels: 90 us -> 65.2 us  [run_middle(): pl.pallas_call(functools.partial(middle_kernel, group, cols, cap), out_sh...]
    all_to_all x2 -> x1, starting transfers between devices: 11.3 us -> 4.66 us  [device_step(): got = lax.all_to_all(held, 'ep', 0, 0, tiled=True)]
    slice x2 -> x0, local copies, waits for them, and re-layouts: 4.98 us -> none  [the longest x1 3.3 us: device_step(): cut1 = later.reshape(layers, slots, 3, 2, part // 2, width)[1]]
    all_to_all x2 -> x1, waiting for transfers between devices: 0.01 us -> 4.79 us  [device_step(): got = lax.all_to_all(held, 'ep', 0, 0, tiled=True)]
    dot_general x1 -> x0, matrix products: 4.75 us -> none  [device_step(): jnp.dot(pick, x_in, preferred_element_type=F32).astype(BF16)]
    select_n x2 -> x1, other arithmetic: 4.44 us -> 0.01 us  [device_step(): held = held[source].reshape(group, slots, depth, width)]
  transfers between devices with their start and end apart: 5 -> 2, of which waited for: 1 -> 1; matrix products, arithmetic and copies ran while one was open for 3% -> 4% of each run, Pallas kernels for 71% -> 35%
where the time goes in v4:
time: 371 us; the launch traced here: 368 us
  Pallas kernels  322 us (87%)
  local copies, waits for them, and re-layouts  20.3 us (5%)
  starting transfers between devices  10.6 us (3%)
  other arithmetic  7.89 us (2%)
  waiting for transfers between devices  4.79 us (1%)
    pallas_call x2, Pallas kernels, run_expert(): pl.pallas_call(functools.partial(expert_kernel, group, cols, wide), out_s...  129 us
    pallas_call x1, Pallas kernels, run_front(): pl.pallas_call(functools.partial(front_kernel, group, cols, cap), out_sha...  82.7 us
    pallas_call x1, Pallas kernels, run_middle(): pl.pallas_call(functools.partial(middle_kernel, group, cols, cap), out_sh...  65.2 us
    pallas_call x1, Pallas kernels, run_last(): pl.pallas_call(functools.partial(last_kernel, group, cols, side, cap), ou...  44.8 us
  transfers between devices with their start and end apart: 2, of which 1 were waited for; matrix products, arithmetic and copies ran while one was open for 4% of the time, Pallas kernels for 35%

profile of v4, /device:TPU:1, one launch (start us, length us, event | category | flops | bytes accessed | tf_op | source)
XLA Modules:
  0.0 368.3 jit_solution(6468346799786841150)
XLA Ops:
  0.6 0.0 copy-start
  0.6 2.6 pad_maximum_fusion
  3.3 2.5 copy.22
  5.8 0.0 copy-start.7
  5.8 0.0 copy-start.5
  5.8 0.0 copy-start.2
  5.8 6.0 %all-to-all-start = ((bf16[8,8,24,1536]{3,2,1,0:T(8,128)(2,1)}), bf16[8,8,24,1536]{3,2,1,0:T(8,128)(2,1)}, u32[]{:S(2)}, u32[]{:S(2)}) async-start(bf16[8,8,24,1536]{3,2,1,0:T(8,128)(2,1)} %bitcast.69), calls=%async_computation | async-start | bytes 9437184 | tf_op jit(solution)/shard_map/all_to_all | solution.py:366
  11.8 1.2 constant_dynamic-slice_fusion.1
  12.9 0.8 copy.26
  13.8 0.0 copy-done
  13.8 0.0 copy-done.7
  13.8 0.7 scatter_fusion
  14.5 0.0 copy-done.5
  14.5 0.1 select_reduce_fusion.4
  14.6 0.0 copy-done.2
  14.7 0.0 copy-start.6
  14.7 0.0 copy-start.4
  14.7 1.0 fusion.2
  15.7 0.1 broadcast_compare_fusion
  15.7 1.1 broadcast_add_fusion.2
  16.8 0.1 select_reduce_fusion.3
  16.9 0.6 broadcast_add_fusion.3.picked_ref
  17.6 0.0 copy-start.3
  17.6 82.7 %shard_map.120 = (bf16[8,128,1536]{2,1,0:T(8,128)(2,1)}, bf16[16,3,16,1536]{3,2,1,0:T(8,128)(2,1)}, bf16[16,3,16,1536]{3,2,1,0:T(8,128)(2,1)}, bf16[16,3,16,1536...) custom-call(bf16[1024,1536]{1,0:T(8,128)(2,1)} %x_ref.1, s32[4,1024]{1,0:T(4,128)} %broadcast_add_fusion.3.picked_ref, ...), custom_call_target="tpu_custom_call" | custom-call | bytes 251658240 | tf_op jit(solution)/shard_map/pallas_call | solution.py:119
  100.2 0.0 copy-done.6
  100.3 0.0 copy-done.3
  100.3 1.5 select_reduce_fusion.1
  101.8 0.0 copy-done.4
  101.8 0.1 iota_compare_fusion.13
  101.9 1.1 broadcast_add_fusion.1
  103.0 1.0 select_reduce_fusion
  104.0 0.7 broadcast_add_fusion.nrank_ref
  104.7 0.0 all-to-all-done
  104.7 5.3 %gather_fusion = bf16[64,24,1536]{2,1,0:T(8,128)(2,1)} fusion(bf16[64,24,1536]{2,1,0:T(8,128)(2,1)} %bitcast.15, s32[1024]{0:T(1024)S(1)} %pad_clamp_fusion), kind=kCustom, calls=%fused_computation | custom fusion | bytes 9437440 | tf_op jit(solution)/shard_map/gather | solution.py:371
  110.0 60.5 %shard_map.121.back_ref = bf16[128,96,128]{2,1,0:T(8,128)(2,1)} custom-call(bf16[8,128,1536]{2,1,0:T(8,128)(2,1)} %get-tuple-element.18.rows_ref, bf16[16,3,16,1536]{3,2,1,0:T(8,128)(2,1)} %get-tuple-element.19.mine_ref, bf16[16,3,16,1536]{3,2,1,0:T(8,128)(2,1)} %get-tuple-element.20.other_ref), custom_call_target="tpu_custom_call" | custom-call | flops 4831838208 | bytes 125829120 | tf_op jit(solution)/shard_map/pallas_call | solution.py:185
  170.5 65.2 %shard_map.122 = (bf16[96,1024]{1,0:T(8,128)(2,1)}, bf16[128,96,128]{2,1,0:T(8,128)(2,1)}) custom-call(s32[40]{0:T(128)} %copy-done.6, bf16[128,96,128]{2,1,0:T(8,128)(2,1)} %shard_map.121.back_ref, s32[40,1024]{1,0:T(8,128)} %get-tuple-element.38.rank_ref, f32[40,1024]{1,0:T(8,128)} %get-tuple-element.44.gate_ref, s32[64,1024]{1,0:T(8,128)} %broadcast_add_fusion.nrank_ref, ...), custom_call_target="tpu_custom_call" | custom-call | flops 5368709120 | bytes 125829120 | tf_op jit(solution)/shard_map/pallas_call | solution.py:260
  235.7 68.6 %shard_map.123.back_ref = bf16[128,96,128]{2,1,0:T(8,128)(2,1)} custom-call(bf16[8,1536,128]{2,1,0:T(8,128)(2,1)} %bitcast.82, bf16[16,3,16,1536]{3,2,1,0:T(8,128)(2,1)} %get-tuple-element.22.mine_ref, bf16[16,3,16,1536]{3,2,1,0:T(8,128)(2,1)} %get-tuple-element.23.other_ref), custom_call_target="tpu_custom_call" | custom-call | flops 4831838208 | bytes 125829120 | tf_op jit(solution)/shard_map/pallas_call | solution.py:185
  304.3 4.7 %all-to-all-start.1 = ((bf16[8,8,24,1536]{3,2,1,0:T(8,128)(2,1)}), bf16[8,8,24,1536]{3,2,1,0:T(8,128)(2,1)}, u32[]{:S(2)}, u32[]{:S(2)}) async-start(bf16[8,8,24,1536]{3,2,1,0:T(8,128)(2,1)} %bitcast.70), calls=%async_computation.1 | async-start | bytes 9437184 | tf_op jit(solution)/shard_map/all_to_all | solution.py:382
  309.0 44.8 %shard_map.124 = bf16[4,4,96,1024]{3,2,1,0:T(8,128)(2,1)} custom-call(s32[40]{0:T(128)} %copy-done.4, bf16[128,96,128]{2,1,0:T(8,128)(2,1)} %shard_map.123.back_ref, s32[40,1024]{1,0:T(8,128)} %get-tuple-element.40.rank_ref, f32[40,1024]{1,0:T(8,128)} %get-tuple-element.43.gate_ref, bf16[96,1024]{1,0:T(8,128)(2,1)} %get-tuple-element.26.res_ref), custom_call_target="tpu_custom_call" | custom-call | flops 5368709120 | bytes 125829120 | tf_op jit(solution)/shard_map/pallas_call | solution.py:309
  353.8 4.6 %copy.24 = bf16[1536,1024]{0,1:T(8,128)(2,1)} copy(bf16[1536,1024]{1,0:T(8,128)(2,1)} %bitcast.80) | data formatting | bytes 6291456 | tf_op jit(solution)/shard_map/reshape | solution.py:383
  358.4 4.8 %all-to-all-done.1 = bf16[8,8,24,1536]{3,2,1,0:T(8,128)(2,1)} async-done(((bf16[8,8,24,1536]{3,2,1,0:T(8,128)(2,1)}), bf16[8,8,24,1536]{3,2,1,0:T(8,128)(2,1)}, u32[]{:S(2)}, u32[]{:S(2)}) %all-to-all-start.1) | async-done | bytes 4718624 | tf_op jit(solution)/shard_map/all_to_all | solution.py:382
  363.2 2.8 copy.25
  366.0 0.0 copy-start.1
  366.0 2.3 slice_bitcast_fusion
  368.3 0.0 copy-done.1
  (9 shorter events, 0.1 us)
Async XLA Ops:
  0.6 13.1 %copy-start = (s32[2,32]{1,0:T(2,128)S(1)}, s32[2,32]{1,0:T(2,128)}, u32[]{:S(2)}) copy-start(s32[2,32]{1,0:T(2,128)} %param.16) | copy-start | bytes 772
  5.8 8.0 %copy-start.7 = (s32[2,32]{1,0:T(2,128)S(1)}, s32[2,32]{1,0:T(2,128)}, u32[]{:S(2)}) copy-start(s32[2,32]{1,0:T(2,128)} %param.17) | copy-start | bytes 772
  5.8 8.7 %copy-start.5 = (s32[2,64]{1,0:T(2,128)S(1)}, s32[2,64]{1,0:T(2,128)}, u32[]{:S(2)}) copy-start(s32[2,64]{1,0:T(2,128)} %param.15) | copy-start | bytes 1540
  5.8 8.9 %copy-start.2 = (s32[2,1024,8]{1,2,0:T(8,128)S(1)}, s32[2,1024,8]{1,2,0:T(8,128)}, u32[]{:S(2)}) copy-start(s32[2,1024,8]{1,2,0:T(8,128)} %param.10) | copy-start | bytes 196612
  5.8 98.9 %all-to-all-start = ((bf16[8,8,24,1536]{3,2,1,0:T(8,128)(2,1)}), bf16[8,8,24,1536]{3,2,1,0:T(8,128)(2,1)}, u32[]{:S(2)}, u32[]{:S(2)}) async-start(bf16[8,8,24,1536]{3,2,1,0:T(8,128)(2,1)} %bitcast.69), calls=%async_computation | async-start | bytes 9437184 | tf_op jit(solution)/shard_map/all_to_all | solution.py:366
  14.7 85.6 %copy-start.6 = (s32[40]{0:T(128)}, s32[40]{0:T(128)S(1)}, u32[]{:S(2)}) copy-start(s32[40]{0:T(128)S(1)} %get-tuple-element.41.first_ref) | copy-start | bytes 484
  14.7 87.1 %copy-start.4 = (s32[40]{0:T(128)}, s32[40]{0:T(128)S(1)}, u32[]{:S(2)}) copy-start(s32[40]{0:T(128)S(1)} %get-tuple-element.42.first_ref) | copy-start | bytes 484
  17.6 82.7 %copy-start.3 = (f32[2,1024,8]{1,2,0:T(8,128)S(1)}, f32[2,1024,8]{1,2,0:T(8,128)}, u32[]{:S(2)}) copy-start(f32[2,1024,8]{1,2,0:T(8,128)} %param.11) | copy-start | bytes 196612
  304.3 58.9 %all-to-all-start.1 = ((bf16[8,8,24,1536]{3,2,1,0:T(8,128)(2,1)}), bf16[8,8,24,1536]{3,2,1,0:T(8,128)(2,1)}, u32[]{:S(2)}, u32[]{:S(2)}) async-start(bf16[8,8,24,1536]{3,2,1,0:T(8,128)(2,1)} %bitcast.70), calls=%async_computation.1 | async-start | bytes 9437184 | tf_op jit(solution)/shard_map/all_to_all | solution.py:382
  366.0 2.3 copy-start.1

commit v5 on v4

v5 whole, which is shorter than its diff:
```python
import functools

import jax
import jax.numpy as jnp
from jax import lax
from jax.experimental import pallas as pl
from jax.experimental.pallas import tpu as pltpu
from jax.sharding import PartitionSpec as P

EXPERTS = 40
F32 = jnp.float32
BF16 = jnp.bfloat16
VMEM = pl.BlockSpec(memory_space=pltpu.VMEM)
SMEM = pl.BlockSpec(memory_space=pltpu.SMEM)
ANY = pl.BlockSpec(memory_space=pl.ANY)
MESH = pl.DeviceIdType.MESH
DMA = pltpu.SemaphoreType.DMA


def params(collective):
    return pltpu.CompilerParams(has_side_effects=True, collective_id=collective)


def signal_all(group, cols):
    ep, tp = lax.axis_index('ep'), lax.axis_index('tp')
    barrier = pltpu.get_barrier_semaphore()

    def tell(k, carry):
        peer = {'tp': lax.rem(tp + k // group, cols), 'ep': lax.rem(ep + lax.rem(k, group), group)}
        pl.semaphore_signal(barrier, inc=1, device_id=peer, device_id_type=MESH)
        return carry

    lax.fori_loop(1, group * cols, tell, 0)


def wait_all(group, cols):
    pl.semaphore_wait(pltpu.get_barrier_semaphore(), group * cols - 1)


def post(src, dst, to_ep, to_tp, send_sem, recv_sem):
    ep, tp = lax.axis_index('ep'), lax.axis_index('tp')
    here = jnp.logical_and(to_ep == ep, to_tp == tp)

    @pl.when(jnp.logical_not(here))
    def _():
        pltpu.make_async_remote_copy(src, dst, send_sem, recv_sem, device_id={'tp': to_tp, 'ep': to_ep}, device_id_type=MESH).start()

    @pl.when(here)
    def _():
        pltpu.make_async_copy(src, dst, recv_sem).start()


def await_bytes(ref, sem):
    pltpu.make_async_copy(ref, ref, sem).wait()


def front_kernel(group, cols, cap, x_ref, picked_ref, g_ref, u_ref, d_ref, rows_ref, mine0_ref, other0_ref, mine1_ref, other1_ref, send_ref, rsend, rrecv, wsend, wrecv, osend, orecv):
    ep, tp = lax.axis_index('ep'), lax.axis_index('tp')
    core = lax.rem(ep, 2)
    slots = g_ref.shape[1]
    half = cap // 2
    mines, others = (mine0_ref, mine1_ref), (other0_ref, other1_ref)
    signal_all(group, cols)
    row_iota = lax.broadcasted_iota(jnp.int32, (cap, x_ref.shape[0]), 0)

    def compute(i, carry):
        pick = (picked_ref[pl.ds(i, 1), :] == row_iota).astype(BF16)
        rows = jnp.dot(pick, x_ref[...], preferred_element_type=F32).astype(BF16)
        send_ref[2 * i] = rows[:half]
        send_ref[2 * i + 1] = rows[half:]
        return carry

    lax.fori_loop(0, group // 2, compute, 0)
    wait_all(group, cols)

    def weights(layer):
        def one(k, carry):
            slot = lax.rem(tp + k // 2, slots)
            part = lax.rem(k, 2)
            for mat, ref in enumerate((g_ref, u_ref, d_ref)):
                post(ref.at[layer, slot, part], mines[layer].at[tp, mat], ep - core + part, slots * core + slot, wsend.at[layer], wrecv.at[layer])
            return carry

        lax.fori_loop(0, 2 * slots, one, 0)

    def rows(k, carry):
        to = lax.rem(ep + k, group)
        post(send_ref.at[to], rows_ref.at[ep], to, tp, rsend, rrecv)
        return carry

    weights(0)
    lax.fori_loop(0, group, rows, 0)
    weights(1)
    swaps = []
    for layer in range(2):
        await_bytes(mines[layer], wrecv.at[layer])
        swap = pltpu.make_async_remote_copy(mines[layer], others[layer], osend.at[layer], orecv.at[layer], device_id={'ep': ep + 1 - 2 * core}, device_id_type=MESH)
        swap.start()
        swaps.append(swap)
    await_bytes(rows_ref, rrecv)
    await_bytes(rows_ref.at[pl.ds(0, group - 1)], rsend)
    own = tp // slots == core
    for layer in range(2):
        @pl.when(own)
        def _():
            await_bytes(mines[layer].at[pl.ds(0, 2 * slots - 1)], wsend.at[layer])

        @pl.when(jnp.logical_not(own))
        def _():
            await_bytes(mines[layer], wsend.at[layer])

        swaps[layer].wait()


def run_front(x, picked, gates, ups, downs, group, cols, cap, collective):
    _, slots, _, part, width = gates.shape
    piece = jax.ShapeDtypeStruct((cols, 3, part, width), BF16)
    rows = (group, cap // 2, width)
    return pl.pallas_call(
        functools.partial(front_kernel, group, cols, cap),
        out_shape=(jax.ShapeDtypeStruct(rows, BF16),) + (piece,) * 4,
        in_specs=[VMEM] * 2 + [ANY] * 3,
        out_specs=(ANY,) * 5,
        scratch_shapes=[pltpu.VMEM(rows, BF16), DMA, DMA] + [DMA((2,))] * 4,
        compiler_params=params(collective),
        cost_estimate=pl.CostEstimate(flops=0, bytes_accessed=240 << 20, transcendentals=0),
    )(x, picked, gates, ups, downs)


def layers_kernel(group, cols, side, cap, source_ref, rows0_ref, mine0_ref, other0_ref, rank0_ref, gate0_ref, rank1_ref, gate1_ref, res_ref, mine1_hbm, other1_hbm, held_hbm,
                  dst_ref, got_ref, out_ref, send_ref, down_ref, back0_ref, rows1_ref, back1_ref, acc_ref, hid_ref, mine1_ref, other1_ref, held_ref, moves_ref,
                  load_sem, own_sem, osend, orecv, msend, mrecv, gsend, grecv):
    ep, tp = lax.axis_index('ep'), lax.axis_index('tp')
    me = ep * cols + tp
    core = lax.rem(ep, 2)
    here = ep // 2
    planes = group // 2
    width = mine0_ref.shape[3]
    ffn_half = mine0_ref.shape[0] * mine0_ref.shape[2]
    feats, half = out_ref.shape[1:]
    tokens = rank0_ref.shape[1]
    all_slots = rank0_ref.shape[0]
    signal_all(group, cols)
    loads = [pltpu.make_async_copy(a, b, load_sem.at[k]) for k, (a, b) in enumerate(((held_hbm, held_ref), (mine1_hbm, mine1_ref), (other1_hbm, other1_ref)))]
    for load in loads:
        load.start()

    def near(i):
        hop = jnp.where(i == 0, 1, jnp.where(i == 1, planes - 1, jnp.where(i == 2, 2, 0)))
        return lax.rem(here + hop, planes)

    def take_plane(ref, sem, i):
        plane = near(i)
        await_bytes(ref.at[pl.ds(2 * cols * plane, 2 * cols)], sem.at[plane])

    def permute(k, carry):
        moves_ref[k] = held_ref[source_ref[k]]
        return carry

    def send_moves(hop, to_core):
        to = 2 * lax.rem(here + hop, planes) + to_core
        per = all_slots // group
        post(moves_ref.at[pl.ds(to * per, per)], got_ref.at[pl.ds(ep * per, per)], to, tp, msend, mrecv)

    def experts(wide, rows_ref, mine_ref, other_ref, dest_ref, stage, first_send):
        def whole(k):
            return jnp.concatenate([mine_ref[:, k].reshape(ffn_half, width), other_ref[:, k].reshape(ffn_half, width)], axis=0)

        def pair(i):
            return 2 * near(2 * (i // 2)) + lax.rem(i, 2), 2 * near(2 * (i // 2) + 1) + lax.rem(i, 2)

        def compute(i):
            one, two = pair(i)
            if wide:
                rows = jnp.concatenate([rows_ref[pl.ds(one * cols, cols)].reshape(width, half), rows_ref[pl.ds(two * cols, cols)].reshape(width, half)], axis=1)
            else:
                rows = jnp.concatenate([rows_ref[one], rows_ref[two]], axis=0)
            dims = (((1,), (0 if wide else 1,)), ((), ()))
            gate = lax.dot_general(whole(0), rows, dims, preferred_element_type=F32)
            up = lax.dot_general(whole(1), rows, dims, preferred_element_type=F32)
            act = (jax.nn.silu(gate) * up).astype(BF16)
            out = jnp.dot(down_ref[...], act, preferred_element_type=F32).astype(BF16)
            out_ref[pl.ds(one * cols, cols)] = out[:, :half].reshape(cols, feats, half)
            out_ref[pl.ds(two * cols, cols)] = out[:, half:].reshape(cols, feats, half)

        def send(i):
            one, two = pair(i)

            def each(k, carry):
                to_ep = jnp.where(lax.rem(k, 2) == 0, one, two)
                to_tp = lax.rem(tp + k // 2, cols)
                post(out_ref.at[to_ep * cols + to_tp], dest_ref.at[me], to_ep, to_tp, osend.at[stage], orecv.at[stage, here])
                return carry

            lax.fori_loop(0, 2 * cols, each, 0)

        down_ref[...] = whole(2).T
        if wide:
            take_plane(rows_ref, orecv.at[1], 0)
            take_plane(rows_ref, orecv.at[1], 1)
        compute(0)
        first_send()
        compute(1)
        send(0)
        if wide:
            take_plane(rows_ref, orecv.at[1], 2)
            take_plane(rows_ref, orecv.at[1], 3)
        compute(2)
        send(1)
        compute(3)
        send(2)
        send(3)

    row_iota = lax.broadcasted_iota(jnp.int32, (cap, tokens), 0)

    def combine(back_ref, rank_ref, gate_ref, stage):
        for i in range(planes):
            take_plane(back_ref, orecv.at[stage], i)
            plane = near(i)

            def step(column, carry):
                block = 2 * plane * cols + column
                slot = plane * cols + column
                rows = jnp.concatenate([back_ref[block], back_ref[block + cols]], axis=1)
                pick = (rank_ref[pl.ds(slot, 1), :] == row_iota).astype(BF16)
                chosen = jnp.dot(rows, pick, preferred_element_type=F32)
                acc_ref[...] += gate_ref[pl.ds(slot, 1), :] * chosen
                return carry

            lax.fori_loop(0, cols, step, 0)
        hid_ref[...] = acc_ref[...].astype(BF16)

    everything = pl.ds(0, group * cols - 1)

    acc_ref[...] = res_ref[...].astype(F32)
    loads[0].wait()
    lax.fori_loop(0, all_slots, permute, 0)

    def first_send():
        wait_all(group, cols)
        send_moves(1, 0)
        send_moves(planes - 1, 0)

    experts(False, rows0_ref, mine0_ref, other0_ref, back0_ref, 0, first_send)
    combine(back0_ref, rank0_ref, gate0_ref, 0)
    await_bytes(back0_ref.at[everything], osend.at[0])
    send_moves(1, 1)
    send_moves(planes - 1, 1)

    def place(i):
        plane = near(2 * (i // (2 * cols)) + lax.rem(i, 2))
        return plane, lax.rem(tp + lax.rem(i, 2 * cols) // 2, cols)

    def choose(i):
        plane, column = place(i)
        pick = (rank1_ref[pl.ds(plane * cols + column, 1), :] == row_iota).astype(BF16)
        rows = lax.dot_general(hid_ref[...], pick, (((1,), (1,)), ((), ())), preferred_element_type=F32).astype(BF16)
        block = 2 * plane * cols + column
        send_ref[block] = rows[:, :half]
        send_ref[block + cols] = rows[:, half:]

    def ship(i):
        plane, column = place(i)
        block = 2 * plane * cols + column
        post(send_ref.at[block], rows1_ref.at[me], 2 * plane, column, osend.at[1], orecv.at[1, here])
        post(send_ref.at[block + cols], rows1_ref.at[me], 2 * plane + 1, column, osend.at[1], orecv.at[1, here])

    choose(0)

    def step(i, carry):
        choose(i)
        ship(i - 1)
        return carry

    lax.fori_loop(1, all_slots, step, 0)
    loads[1].wait()
    loads[2].wait()
    ship(all_slots - 1)
    acc_ref[...] = hid_ref[...].astype(F32)
    experts(True, rows1_ref, mine1_ref, other1_ref, back1_ref, 2, lambda: None)
    for to_core in range(2):
        send_moves(2, to_core)
        send_moves(0, to_core)
    combine(back1_ref, rank1_ref, gate1_ref, 2)

    z, y = tp // side, lax.rem(tp, side)
    cut = feats // 2
    low, high = pl.ds(0, cut), pl.ds(cut, cut)
    await_bytes(back0_ref.at[everything], osend.at[1])
    await_bytes(back0_ref.at[everything], osend.at[2])
    own = pltpu.make_async_copy(hid_ref, dst_ref.at[z, y], own_sem)
    own.start()
    own.wait()

    def push(ref, to_z, to_y, k):
        pltpu.make_async_remote_copy(ref, ref, gsend.at[k], grecv.at[k], device_id={'tp': to_z * side + to_y}, device_id_type=MESH).start()

    for j in range(1, side):
        push(dst_ref.at[z, y, low], z, lax.rem(y + j, side), 0)
        push(dst_ref.at[z, y, high], lax.rem(z + j, side), y, 1)
    some = pl.ds(0, side - 1)
    await_bytes(dst_ref.at[z, some, low], grecv.at[0])
    for j in range(1, side):
        push(dst_ref.at[z, :, low], lax.rem(z + j, side), y, 2)
    await_bytes(dst_ref.at[some, y, high], grecv.at[1])
    for j in range(1, side):
        push(dst_ref.at[:, y, high], z, lax.rem(y + j, side), 3)
    await_bytes(dst_ref.at[some, :, low], grecv.at[2])
    await_bytes(dst_ref.at[:, some, high], grecv.at[3])
    await_bytes(dst_ref.at[z, some, low], gsend.at[0])
    await_bytes(dst_ref.at[some, y, high], gsend.at[1])
    await_bytes(dst_ref.at[some, :, low], gsend.at[2])
    await_bytes(dst_ref.at[:, some, high], gsend.at[3])
    await_bytes(got_ref, mrecv)
    await_bytes(got_ref.at[pl.ds(0, all_slots - all_slots // group)], msend)


def run_layers(source, rows, w0, tables, residual, w1, held, group, cols, cap, collective):
    feats, tokens = residual.shape
    side = int(round(cols ** 0.5))
    piece = w0[0].shape
    width = piece[3]
    ffn = 2 * piece[0] * piece[2]
    blocks = pltpu.VMEM((group * cols, feats, cap // 2), BF16)
    return pl.pallas_call(
        functools.partial(layers_kernel, group, cols, side, cap),
        out_shape=(jax.ShapeDtypeStruct((side, side, feats, tokens), BF16), jax.ShapeDtypeStruct(held.shape, BF16)),
        in_specs=[SMEM] + [VMEM] * 8 + [ANY] * 3,
        out_specs=(ANY, ANY),
        scratch_shapes=[blocks, blocks, pltpu.VMEM((width, ffn), BF16), blocks, blocks, blocks, pltpu.VMEM((feats, tokens), F32), pltpu.VMEM((feats, tokens), BF16),
                        pltpu.VMEM(piece, BF16), pltpu.VMEM(piece, BF16), pltpu.VMEM(held.shape, BF16), pltpu.VMEM(held.shape, BF16),
                        DMA((3,)), DMA, DMA((3,)), DMA((3, group // 2)), DMA, DMA, DMA((4,)), DMA((4,))],
        compiler_params=pltpu.CompilerParams(has_side_effects=True, collective_id=collective, vmem_limit_bytes=60 << 20),
        cost_estimate=pl.CostEstimate(flops=40 << 30, bytes_accessed=480 << 20, transcendentals=0),
    )(source, rows, *w0, *tables, residual, *w1, held)


def solution(mesh):
    group = mesh.shape['ep']
    cols = mesh.shape['tp']
    row_spec = P(('rep', 'ep'), None)
    layer_spec = P(None, ('rep', 'ep'), None)
    col_spec = P(None, ('rep', 'ep'), None, 'tp')
    down_spec = P(None, ('rep', 'ep'), 'tp', None)
    map_spec = P(None, None)

    def device_step(x_in, route_ids, gate_vals, w_gate, w_up, w_down, old_map, move_src, move_dst):
        layers, slots, width, part = w_gate.shape
        tokens, top_k = route_ids.shape[1], route_ids.shape[2]
        all_slots = group * slots
        cap = 2 * tokens * top_k // all_slots
        half = cap // 2
        feats = width // cols
        ep = lax.axis_index('ep')
        tp = lax.axis_index('tp')

        tables = []
        expert_ids = jnp.arange(EXPERTS, dtype=jnp.int32)
        slot_ids = jnp.arange(all_slots, dtype=jnp.int32)
        before = (jnp.arange(tokens)[:, None] < jnp.arange(tokens)[None, :]).astype(BF16)
        for layer in range(layers):
            ids = route_ids[layer].T
            match = ids[None, :, :] == expert_ids[:, None, None]
            taken = jnp.any(match, axis=1)
            gate = jnp.sum(jnp.where(match, gate_vals[layer].T[None], 0.0), axis=1)
            rank = jnp.dot(taken.astype(BF16), before, preferred_element_type=F32).astype(jnp.int32)
            rank = jnp.where(taken, rank, -1)
            holds = old_map[layer][None, :] == expert_ids[:, None]
            first = jnp.min(jnp.where(holds, slot_ids[None, :], all_slots - 1), axis=1)
            serving = (first[:, None] == slot_ids[None, :])[:, :, None]
            by_slot = jnp.sum(jnp.where(serving, rank[:, None, :] + 1, 0), axis=0) - 1
            gate_slot = jnp.sum(jnp.where(serving, gate[:, None, :], 0.0), axis=0)
            tables.append((by_slot, gate_slot, rank, first))

        _, _, rank, first = tables[0]
        my_slots = jnp.arange(group // 2, dtype=jnp.int32) * cols + tp
        serves = first[:, None] == my_slots[None, :]
        picked = jnp.sum(jnp.where(serves[:, :, None], rank[:, None, :] + 1, 0), axis=0) - 1
        cut = (layers, slots, 2, part // 2, width)
        w_g, w_u = jnp.swapaxes(w_gate, 2, 3), jnp.swapaxes(w_up, 2, 3)
        rows, mine, other, mine1, other1 = run_front(x_in, picked, w_g.reshape(cut), w_u.reshape(cut), w_down.reshape(cut), group, cols, cap, 0)

        pieces = group // layers
        depth = 3 * part // pieces
        packed = jnp.stack([w_g, w_u, w_down], axis=2)
        cut2 = packed.reshape(layers, slots, pieces, depth, width).transpose(0, 2, 1, 3, 4).reshape(group, slots, depth, width)
        held = lax.all_to_all(cut2, 'ep', 0, 0, tiled=True).reshape(all_slots, depth, width)
        source = jnp.arange(all_slots, dtype=jnp.int32)
        my_layer = ep // pieces
        source = source.at[move_dst[my_layer]].set(move_src[my_layer])
        residual = lax.dynamic_slice_in_dim(x_in, tp * feats, feats, axis=1).T
        y_out, got = run_layers(source, rows, (mine, other), tables[0][:2] + tables[1][:2], residual, (mine1, other1), held, group, cols, cap, 1)
        y_out = y_out.reshape(width, tokens).T

        new = got.reshape(layers, pieces, slots, depth, width).transpose(0, 2, 1, 3, 4).reshape(layers, slots, 3, part, width)
        return y_out, jnp.swapaxes(new[:, :, 0], 2, 3), jnp.swapaxes(new[:, :, 1], 2, 3), new[:, :, 2]

    return jax.shard_map(device_step, mesh=mesh, in_specs=(row_spec, layer_spec, layer_spec, col_spec, col_spec, down_spec, map_spec, map_spec, map_spec), out_specs=(row_spec, col_spec, col_spec, down_spec), check_vma=False)
```

time: 371 us -> 350 us (0.943)
  the two profiles are of different devices: /device:TPU:1 before, /device:TPU:7 now
where the time goes in v5:
time: 350 us; the launch traced here: 349 us
  Pallas kernels  315 us (90%)
  local copies, waits for them, and re-layouts  15 us (4%)
  other arithmetic  12.6 us (4%)
  starting transfers between devices  5.25 us (2%)
    pallas_call x1, Pallas kernels, run_layers(): pl.pallas_call(functools.partial(layers_kernel, group, cols, side, cap),...  235 us
    pallas_call x1, Pallas kernels, run_front(): pl.pallas_call(functools.partial(front_kernel, group, cols, cap), out_sha...  80 us
  transfers between devices with their start and end apart: 1, of which 0 were waited for; matrix products, arithmetic and copies ran while one was open for 4% of the time, Pallas kernels for 23%

profile of v5, /device:TPU:7, one launch (start us, length us, event | category | flops | bytes accessed | tf_op | source)
XLA Modules:
  0.0 349.4 jit_solution(3257454800401340376)
XLA Ops:
  0.6 0.0 copy-start
  0.6 2.6 pad_maximum_fusion
  3.3 2.6 copy.23
  5.8 0.0 copy-start.4
  5.8 0.0 copy-start.5
  5.8 0.0 copy-start.2
  5.8 5.2 %all-to-all-start = ((bf16[8,8,24,1536]{3,2,1,0:T(8,128)(2,1)}), bf16[8,8,24,1536]{3,2,1,0:T(8,128)(2,1)}, u32[]{:S(2)}, u32[]{:S(2)}) async-start(bf16[8,8,24,1536]{3,2,1,0:T(8,128)(2,1)} %bitcast.67), calls=%async_computation | async-start | bytes 9437184 | tf_op jit(solution)/shard_map/all_to_all | solution.py:387
  11.1 0.0 copy-done.4
  11.1 0.0 copy-done
  11.2 1.2 constant_dynamic-slice_fusion
  12.3 0.0 copy-done.5
  12.4 0.8 copy.26
  13.2 0.7 scatter_fusion
  13.9 0.0 copy-start.1
  13.9 0.1 select_reduce_fusion.7
  14.0 0.0 copy-done.2
  14.0 1.0 fusion.2
  15.0 0.1 broadcast_compare_fusion
  15.1 0.4 fusion.6
  15.5 0.1 select_reduce_fusion.6
  15.6 0.6 broadcast_add_fusion.2.picked_ref
  16.3 0.0 copy-start.3
  16.3 80.0 %shard_map.120 = (bf16[8,128,1536]{2,1,0:T(8,128)(2,1)}, bf16[16,3,16,1536]{3,2,1,0:T(8,128)(2,1)}, bf16[16,3,16,1536]{3,2,1,0:T(8,128)(2,1)}, bf16[16,3,16,1536...) custom-call(bf16[1024,1536]{1,0:T(8,128)(2,1)} %x_ref.1, s32[4,1024]{1,0:T(4,128)} %broadcast_add_fusion.2.picked_ref, ...), custom_call_target="tpu_custom_call" | custom-call | bytes 251658240 | tf_op jit(solution)/shard_map/pallas_call | solution.py:119
  96.3 0.0 copy-done.1
  96.3 0.0 copy-done.3
  96.3 0.8 select_reduce_fusion.4
  97.2 0.1 iota_compare_fusion.19
  97.2 0.1 iota_compare_fusion.17
  97.3 0.4 fusion.9
  97.7 1.0 select_reduce_fusion.1
  98.8 0.7 broadcast_add_fusion.rank1_ref
  99.5 1.1 select_reduce_fusion.3
  100.6 0.7 broadcast_add_fusion.1.rank0_ref
  101.3 1.7 select_reduce_fusion.gate1_ref
  103.0 1.7 select_reduce_fusion.2.gate0_ref
  104.8 0.0 all-to-all-done
  104.8 234.9 %shard_map.121 = (bf16[4,4,96,1024]{3,2,1,0:T(8,128)(2,1)}, bf16[64,24,1536]{2,1,0:T(8,128)(2,1)}) custom-call(s32[64]{0:T(128)} %copy-done.1, bf16[8,128,1536]{2,1,0:T(8,128)(2,1)} %get-tuple-element.11.rows0_ref, bf16[16,3,16,1536]{3,2,1,0:T(8,128)(2,1)} %get-tuple-element.12.mine0_ref, bf16[16,3,16,1536]{3,2,1,0:T(8,128)(2,1)} %get-tuple-element.13.other0_ref, ...), custom_call_target="tpu_custom_call" | custom-call | flops 42949672960 | bytes 503316480 | tf_op jit(solution)/shard_map/pallas_call | solution.py:325
  339.6 4.6 %copy.24 = bf16[1536,1024]{0,1:T(8,128)(2,1)} copy(bf16[1536,1024]{1,0:T(8,128)(2,1)} %bitcast.78) | data formatting | bytes 6291456 | tf_op jit(solution)/shard_map/reshape | solution.py:393
  344.3 2.8 copy.25
  347.1 2.3 slice_bitcast_fusion
  (7 shorter events, 0.0 us)
Async XLA Ops:
  0.6 10.5 %copy-start = (s32[2,32]{1,0:T(2,128)S(1)}, s32[2,32]{1,0:T(2,128)}, u32[]{:S(2)}) copy-start(s32[2,32]{1,0:T(2,128)} %param.16) | copy-start | bytes 772
  5.8 5.3 %copy-start.4 = (s32[2,64]{1,0:T(2,128)S(1)}, s32[2,64]{1,0:T(2,128)}, u32[]{:S(2)}) copy-start(s32[2,64]{1,0:T(2,128)} %param.15) | copy-start | bytes 1540
  5.8 6.5 %copy-start.5 = (s32[2,32]{1,0:T(2,128)S(1)}, s32[2,32]{1,0:T(2,128)}, u32[]{:S(2)}) copy-start(s32[2,32]{1,0:T(2,128)} %param.17) | copy-start | bytes 772
  5.8 8.2 %copy-start.2 = (s32[2,1024,8]{1,2,0:T(8,128)S(1)}, s32[2,1024,8]{1,2,0:T(8,128)}, u32[]{:S(2)}) copy-start(s32[2,1024,8]{1,2,0:T(8,128)} %param.10) | copy-start | bytes 196612
  5.8 98.9 %all-to-all-start = ((bf16[8,8,24,1536]{3,2,1,0:T(8,128)(2,1)}), bf16[8,8,24,1536]{3,2,1,0:T(8,128)(2,1)}, u32[]{:S(2)}, u32[]{:S(2)}) async-start(bf16[8,8,24,1536]{3,2,1,0:T(8,128)(2,1)} %bitcast.67), calls=%async_computation | async-start | bytes 9437184 | tf_op jit(solution)/shard_map/all_to_all | solution.py:387
  13.9 82.4 %copy-start.1 = (s32[64]{0:T(128)}, s32[64]{0:T(128)S(1)}, u32[]{:S(2)}) copy-start(s32[64]{0:T(128)S(1)} %scatter_fusion) | copy-start | bytes 772
  16.3 80.0 %copy-start.3 = (f32[2,1024,8]{1,2,0:T(8,128)S(1)}, f32[2,1024,8]{1,2,0:T(8,128)}, u32[]{:S(2)}) copy-start(f32[2,1024,8]{1,2,0:T(8,128)} %param.11) | copy-start | bytes 196612

commit v6 on v5

v6 whole, which is shorter than its diff:
```python
import functools

import jax
import jax.numpy as jnp
from jax import lax
from jax.experimental import pallas as pl
from jax.experimental.pallas import tpu as pltpu
from jax.sharding import PartitionSpec as P

EXPERTS = 40
F32 = jnp.float32
BF16 = jnp.bfloat16
VMEM = pl.BlockSpec(memory_space=pltpu.VMEM)
SMEM = pl.BlockSpec(memory_space=pltpu.SMEM)
ANY = pl.BlockSpec(memory_space=pl.ANY)
MESH = pl.DeviceIdType.MESH
DMA = pltpu.SemaphoreType.DMA


def params(collective):
    return pltpu.CompilerParams(has_side_effects=True, collective_id=collective)


def signal_all(group, cols):
    ep, tp = lax.axis_index('ep'), lax.axis_index('tp')
    barrier = pltpu.get_barrier_semaphore()

    def tell(k, carry):
        peer = {'tp': lax.rem(tp + k // group, cols), 'ep': lax.rem(ep + lax.rem(k, group), group)}
        pl.semaphore_signal(barrier, inc=1, device_id=peer, device_id_type=MESH)
        return carry

    lax.fori_loop(1, group * cols, tell, 0)


def wait_all(group, cols):
    pl.semaphore_wait(pltpu.get_barrier_semaphore(), group * cols - 1)


def post(src, dst, to_ep, to_tp, send_sem, recv_sem):
    ep, tp = lax.axis_index('ep'), lax.axis_index('tp')
    here = jnp.logical_and(to_ep == ep, to_tp == tp)

    @pl.when(jnp.logical_not(here))
    def _():
        pltpu.make_async_remote_copy(src, dst, send_sem, recv_sem, device_id={'tp': to_tp, 'ep': to_ep}, device_id_type=MESH).start()

    @pl.when(here)
    def _():
        pltpu.make_async_copy(src, dst, recv_sem).start()


def await_bytes(ref, sem):
    pltpu.make_async_copy(ref, ref, sem).wait()


def layers_kernel(group, cols, side, cap, source_ref, sexp_ref, ids_ref, gates_ref, x_ref, res_ref, g16, u16, d16, g8, u8, d8,
                  dst_ref, newg_ref, newu_ref, newd_ref, rank0_ref, gate0_ref, rank1_ref, gate1_ref, rsend_ref, rows0_ref, mine0_ref, other0_ref, mine1_ref, other1_ref,
                  out_ref, send_ref, down_ref, back0_ref, rows1_ref, back1_ref, acc_ref, hid_ref, held_ref, moves_ref,
                  own_sem, rsend, rrecv, wsend, wrecv, ssend, srecv, hsend, hrecv, msend, mrecv, osend, orecv, gsend, grecv):
    ep, tp = lax.axis_index('ep'), lax.axis_index('tp')
    me = ep * cols + tp
    core = lax.rem(ep, 2)
    here = ep // 2
    planes = group // 2
    width = mine0_ref.shape[3]
    ffn_half = mine0_ref.shape[0] * mine0_ref.shape[2]
    feats, half = out_ref.shape[1:]
    all_slots, tokens = rank0_ref.shape
    slots = all_slots // group
    pieces = group // 2
    signal_all(group, cols)
    def near(i):
        hop = jnp.where(i == 0, 1, jnp.where(i == 1, planes - 1, jnp.where(i == 2, 2, 0)))
        return lax.rem(here + hop, planes)

    def take_plane(ref, sem, i):
        plane = near(i)
        per = ref.shape[0] // planes
        await_bytes(ref.at[pl.ds(per * plane, per)], sem.at[plane])

    row_iota = lax.broadcasted_iota(jnp.int32, (cap, tokens), 0)

    def table(layer, rank_ref, gate_ref):
        holds = sexp_ref[layer]
        taken = jnp.zeros((all_slots, tokens), F32)
        gate = jnp.zeros((all_slots, tokens), F32)
        for j in range(ids_ref.shape[1]):
            match = ids_ref[layer, j:j + 1, :] == holds
            taken = jnp.where(match, 1.0, taken)
            gate = jnp.where(match, gates_ref[layer, j:j + 1, :], gate)
        earlier = lax.broadcasted_iota(jnp.int32, (tokens, tokens), 0) < lax.broadcasted_iota(jnp.int32, (tokens, tokens), 1)
        rank = jnp.dot(taken.astype(BF16), earlier.astype(BF16), preferred_element_type=F32).astype(jnp.int32)
        rank_ref[...] = jnp.where(taken > 0.0, rank, -1)
        gate_ref[...] = gate

    def first_rows(i, carry):
        pick = (rank0_ref[pl.ds(i * cols + tp, 1), :] == row_iota).astype(BF16)
        rows = jnp.dot(pick, x_ref[...], preferred_element_type=F32).astype(BF16)
        rsend_ref[2 * i] = rows[:half]
        rsend_ref[2 * i + 1] = rows[half:]
        return carry

    def send_weights(layer, mine_ref):
        def one(k, carry):
            slot = lax.rem(tp + k // 2, slots)
            part = lax.rem(k, 2)
            for mat, ref in enumerate((g16, u16, d16)):
                post(ref.at[layer, slot, part], mine_ref.at[tp, mat], ep - core + part, slots * core + slot, wsend.at[layer], wrecv.at[layer])
            return carry

        lax.fori_loop(0, 2 * slots, one, 0)

    def swap_weights(layer, mine_ref, other_ref):
        await_bytes(mine_ref, wrecv.at[layer])
        swap = pltpu.make_async_remote_copy(mine_ref, other_ref, ssend.at[layer], srecv.at[layer], device_id={'ep': ep + 1 - 2 * core}, device_id_type=MESH)
        swap.start()
        return swap

    def send_rows(k, carry):
        to = 2 * near(k // 2) + lax.rem(k, 2)
        post(rsend_ref.at[to], rows0_ref.at[ep], to, tp, rsend, rrecv.at[here])
        return carry

    def gather_moves(k, carry):
        to = 2 * near(k // 2) + lax.rem(k, 2)
        for mat, ref in enumerate((g8, u8, d8)):
            post(ref.at[to // pieces, :, lax.rem(to, pieces)], held_ref.at[pl.ds(ep * slots, slots), mat], to, tp, hsend, hrecv)
        return carry

    def permute(k, carry):
        moves_ref[k] = held_ref[source_ref[k]]
        return carry

    def send_moves(i, to_core):
        to = 2 * near(i) + to_core
        for mat, ref in enumerate((newg_ref, newu_ref, newd_ref)):
            post(moves_ref.at[pl.ds(to * slots, slots), mat], ref.at[ep // pieces, :, lax.rem(ep, pieces)], to, tp, msend.at[mat], mrecv.at[mat])

    def experts(wide, rows_ref, mine_ref, other_ref, dest_ref, stage):
        def whole(k):
            return jnp.concatenate([mine_ref[:, k].reshape(ffn_half, width), other_ref[:, k].reshape(ffn_half, width)], axis=0)

        def pair(i):
            return 2 * near(2 * (i // 2)) + lax.rem(i, 2), 2 * near(2 * (i // 2) + 1) + lax.rem(i, 2)

        def compute(i):
            one, two = pair(i)
            if wide:
                rows = jnp.concatenate([rows_ref[pl.ds(one * cols, cols)].reshape(width, half), rows_ref[pl.ds(two * cols, cols)].reshape(width, half)], axis=1)
            else:
                rows = jnp.concatenate([rows_ref[one], rows_ref[two]], axis=0)
            dims = (((1,), (0 if wide else 1,)), ((), ()))
            gate = lax.dot_general(whole(0), rows, dims, preferred_element_type=F32)
            up = lax.dot_general(whole(1), rows, dims, preferred_element_type=F32)
            act = (jax.nn.silu(gate) * up).astype(BF16)
            out = jnp.dot(down_ref[...], act, preferred_element_type=F32).astype(BF16)
            out_ref[pl.ds(one * cols, cols)] = out[:, :half].reshape(cols, feats, half)
            out_ref[pl.ds(two * cols, cols)] = out[:, half:].reshape(cols, feats, half)

        def send(i):
            one, two = pair(i)

            def each(k, carry):
                to_ep = jnp.where(lax.rem(k, 2) == 0, one, two)
                to_tp = lax.rem(tp + k // 2, cols)
                post(out_ref.at[to_ep * cols + to_tp], dest_ref.at[me], to_ep, to_tp, osend.at[stage], orecv.at[stage, here])
                return carry

            lax.fori_loop(0, 2 * cols, each, 0)

        down_ref[...] = whole(2).T
        arrived = orecv.at[1] if wide else rrecv
        take_plane(rows_ref, arrived, 0)
        take_plane(rows_ref, arrived, 1)
        compute(0)
        compute(1)
        send(0)
        take_plane(rows_ref, arrived, 2)
        take_plane(rows_ref, arrived, 3)
        compute(2)
        send(1)
        compute(3)
        send(2)
        send(3)

    def combine(back_ref, rank_ref, gate_ref, stage):
        for i in range(planes):
            take_plane(back_ref, orecv.at[stage], i)
            plane = near(i)

            def step(column, carry):
                block = 2 * plane * cols + column
                slot = plane * cols + column
                rows = jnp.concatenate([back_ref[block], back_ref[block + cols]], axis=1)
                pick = (rank_ref[pl.ds(slot, 1), :] == row_iota).astype(BF16)
                chosen = jnp.dot(rows, pick, preferred_element_type=F32)
                acc_ref[...] += gate_ref[pl.ds(slot, 1), :] * chosen
                return carry

            lax.fori_loop(0, cols, step, 0)
        hid_ref[...] = acc_ref[...].astype(BF16)

    everything = pl.ds(0, group * cols - 1)

    table(0, rank0_ref, gate0_ref)
    lax.fori_loop(0, planes, first_rows, 0)
    wait_all(group, cols)
    send_weights(0, mine0_ref)
    lax.fori_loop(0, group, send_rows, 0)
    send_weights(1, mine1_ref)
    lax.fori_loop(0, group, gather_moves, 0)
    table(1, rank1_ref, gate1_ref)
    acc_ref[...] = res_ref[...].astype(F32)
    swap0 = swap_weights(0, mine0_ref, other0_ref)
    swap0.wait_recv()
    experts(False, rows0_ref, mine0_ref, other0_ref, back0_ref, 0)
    swap1 = swap_weights(1, mine1_ref, other1_ref)
    combine(back0_ref, rank0_ref, gate0_ref, 0)
    await_bytes(back0_ref.at[everything], osend.at[0])
    await_bytes(held_ref, hrecv)
    lax.fori_loop(0, all_slots, permute, 0)

    def place(i):
        plane = near(2 * (i // (2 * cols)) + lax.rem(i, 2))
        return plane, lax.rem(tp + lax.rem(i, 2 * cols) // 2, cols)

    def choose(i):
        plane, column = place(i)
        pick = (rank1_ref[pl.ds(plane * cols + column, 1), :] == row_iota).astype(BF16)
        rows = lax.dot_general(hid_ref[...], pick, (((1,), (1,)), ((), ())), preferred_element_type=F32).astype(BF16)
        block = 2 * plane * cols + column
        send_ref[block] = rows[:, :half]
        send_ref[block + cols] = rows[:, half:]

    def ship(i):
        plane, column = place(i)
        block = 2 * plane * cols + column
        post(send_ref.at[block], rows1_ref.at[me], 2 * plane, column, osend.at[1], orecv.at[1, here])
        post(send_ref.at[block + cols], rows1_ref.at[me], 2 * plane + 1, column, osend.at[1], orecv.at[1, here])

    choose(0)
    for to_core in range(2):
        send_moves(0, to_core)
        send_moves(1, to_core)

    def step(i, carry):
        choose(i)
        ship(i - 1)
        return carry

    lax.fori_loop(1, all_slots, step, 0)
    swap1.wait_recv()
    ship(all_slots - 1)
    acc_ref[...] = hid_ref[...].astype(F32)
    experts(True, rows1_ref, mine1_ref, other1_ref, back1_ref, 2)
    for to_core in range(2):
        send_moves(2, to_core)
        send_moves(3, to_core)
    combine(back1_ref, rank1_ref, gate1_ref, 2)

    z, y = tp // side, lax.rem(tp, side)
    cut = feats // 2
    low, high = pl.ds(0, cut), pl.ds(cut, cut)
    await_bytes(back0_ref.at[everything], osend.at[1])
    await_bytes(back0_ref.at[everything], osend.at[2])
    own = pltpu.make_async_copy(hid_ref, dst_ref.at[z, y], own_sem)
    own.start()
    own.wait()

    def push(ref, to_z, to_y, k):
        pltpu.make_async_remote_copy(ref, ref, gsend.at[k], grecv.at[k], device_id={'tp': to_z * side + to_y}, device_id_type=MESH).start()

    for j in range(1, side):
        push(dst_ref.at[z, y, low], z, lax.rem(y + j, side), 0)
        push(dst_ref.at[z, y, high], lax.rem(z + j, side), y, 1)
    some = pl.ds(0, side - 1)
    await_bytes(dst_ref.at[z, some, low], grecv.at[0])
    for j in range(1, side):
        push(dst_ref.at[z, :, low], lax.rem(z + j, side), y, 2)
    await_bytes(dst_ref.at[some, y, high], grecv.at[1])
    for j in range(1, side):
        push(dst_ref.at[:, y, high], z, lax.rem(y + j, side), 3)
    await_bytes(dst_ref.at[some, :, low], grecv.at[2])
    await_bytes(dst_ref.at[:, some, high], grecv.at[3])
    await_bytes(dst_ref.at[z, some, low], gsend.at[0])
    await_bytes(dst_ref.at[some, y, high], gsend.at[1])
    await_bytes(dst_ref.at[some, :, low], gsend.at[2])
    await_bytes(dst_ref.at[:, some, high], gsend.at[3])
    sent = pl.ds(0, all_slots - slots)
    for mat, ref in enumerate((newg_ref, newu_ref, newd_ref)):
        await_bytes(ref, mrecv.at[mat])
        await_bytes(held_ref.at[sent, mat], msend.at[mat])
    await_bytes(held_ref.at[sent], hsend)
    await_bytes(rows0_ref.at[pl.ds(0, group - 1)], rsend)
    own_slot = tp // slots == core
    for layer, (mine_ref, swap) in enumerate(((mine0_ref, swap0), (mine1_ref, swap1))):
        swap.wait_send()

        @pl.when(own_slot)
        def _():
            await_bytes(mine_ref.at[pl.ds(0, cols - 1)], wsend.at[layer])

        @pl.when(jnp.logical_not(own_slot))
        def _():
            await_bytes(mine_ref, wsend.at[layer])


def run_layers(source, holds, ids, gates, x, residual, halves, pieces, group, cols, cap):
    feats, tokens = residual.shape
    width = x.shape[1]
    side = int(round(cols ** 0.5))
    _, slots, _, part, _ = halves[0].shape
    depth = pieces[0].shape[3]
    all_slots = group * slots
    half = cap // 2
    ffn = 2 * cols * part

    def vmem(*shape, dtype=BF16):
        return pltpu.VMEM(shape, dtype)

    weights = vmem(cols, 3, part, width)
    blocks = vmem(group * cols, feats, half)
    rows = vmem(group, half, width)
    held = vmem(all_slots, 3, depth, width)
    return pl.pallas_call(
        functools.partial(layers_kernel, group, cols, side, cap),
        out_shape=(jax.ShapeDtypeStruct((side, side, feats, tokens), BF16),) + (jax.ShapeDtypeStruct(pieces[0].shape, BF16),) * 3,
        in_specs=[SMEM] + [VMEM] * 5 + [ANY] * 6,
        out_specs=(ANY,) * 4,
        scratch_shapes=[vmem(all_slots, tokens, dtype=jnp.int32), vmem(all_slots, tokens, dtype=F32)] * 2 + [rows, rows] + [weights] * 4
                       + [blocks, blocks, vmem(width, ffn), blocks, blocks, blocks, vmem(feats, tokens, dtype=F32), vmem(feats, tokens), held, held,
                          DMA, DMA, DMA((group // 2,)), DMA((2,)), DMA((2,)), DMA((2,)), DMA((2,)), DMA, DMA, DMA((3,)), DMA((3,)), DMA((3,)), DMA((3, group // 2)), DMA((4,)), DMA((4,))],
        compiler_params=pltpu.CompilerParams(has_side_effects=True, collective_id=0, vmem_limit_bytes=62 << 20),
    )(source, holds, ids, gates, x, residual, *halves, *pieces)


def solution(mesh):
    group = mesh.shape['ep']
    cols = mesh.shape['tp']
    row_spec = P(('rep', 'ep'), None)
    layer_spec = P(None, ('rep', 'ep'), None)
    col_spec = P(None, ('rep', 'ep'), None, 'tp')
    down_spec = P(None, ('rep', 'ep'), 'tp', None)
    map_spec = P(None, None)

    def device_step(x_in, route_ids, gate_vals, w_gate, w_up, w_down, old_map, move_src, move_dst):
        layers, slots, width, part = w_gate.shape
        tokens, top_k = route_ids.shape[1], route_ids.shape[2]
        all_slots = group * slots
        cap = 2 * tokens * top_k // all_slots
        half = cap // 2
        feats = width // cols
        ep = lax.axis_index('ep')
        tp = lax.axis_index('tp')

        slot_ids = jnp.arange(all_slots, dtype=jnp.int32)
        again = (old_map[:, :, None] == old_map[:, None, :]) & (slot_ids[None, :] < slot_ids[:, None])[None]
        holds = jnp.where(jnp.any(again, axis=2), -1, old_map)[:, :, None]

        pieces = group // layers
        mine = ep // pieces
        hit = slot_ids[:, None] == move_dst[mine][None, :]
        source = jnp.where(jnp.any(hit, axis=1), jnp.sum(jnp.where(hit, move_src[mine][None, :], 0), axis=1), slot_ids)

        residual = lax.dynamic_slice_in_dim(x_in, tp * feats, feats, axis=1).T
        mats = (jnp.swapaxes(w_gate, 2, 3), jnp.swapaxes(w_up, 2, 3), w_down)
        halves = [m.reshape(layers, slots, 2, part // 2, width) for m in mats]
        groups = [m.reshape(layers, slots, pieces, part // pieces, width) for m in mats]
        y_out, *new = run_layers(source, holds, jnp.swapaxes(route_ids, 1, 2), jnp.swapaxes(gate_vals, 1, 2), x_in, residual, halves, groups, group, cols, cap)
        y_out = y_out.reshape(width, tokens).T
        new = [m.reshape(layers, slots, part, width) for m in new]
        return y_out, jnp.swapaxes(new[0], 2, 3), jnp.swapaxes(new[1], 2, 3), new[2]

    return jax.shard_map(device_step, mesh=mesh, in_specs=(row_spec, layer_spec, layer_spec, col_spec, col_spec, down_spec, map_spec, map_spec, map_spec), out_specs=(row_spec, col_spec, col_spec, down_spec), check_vma=False)
```

time: 350 us -> 329 us (0.940)
  the two profiles are of different devices: /device:TPU:7 before, /device:TPU:1 now
where the time goes in v6:
time: 329 us; the launch traced here: 327 us
  Pallas kernels  310 us (94%)
  local copies, waits for them, and re-layouts  13.3 us (4%)
    pallas_call x1, Pallas kernels, run_layers(): pl.pallas_call(functools.partial(layers_kernel, group, cols, side, cap),...  310 us

profile of v6, /device:TPU:1, one launch (start us, length us, event | category | flops | bytes accessed | tf_op | source)
XLA Modules:
  0.0 326.7 jit_solution(7191925188299496191)
XLA Ops:
  0.7 0.7 fusion.1
  1.4 0.1 select_reduce_fusion
  1.5 0.1 fusion
  1.5 0.5 iota_select_fusion.source_ref
  2.1 0.9 and_reduce_fusion
  3.0 0.7 select_bitcast_fusion
  3.7 0.7 copy.17.sexp_ref
  4.4 1.2 constant_dynamic-slice_fusion
  5.6 0.8 copy.19
  6.4 310.3 %shard_map.120 = (bf16[4,4,96,1024]{3,2,1,0:T(8,128)(2,1)}, bf16[2,8,4,8,1536]{4,3,2,1,0:T(8,128)(2,1)}, bf16[2,8,4,8,1536]{4,3,2,1,0:T(8,128)(2,1)}, bf16[2,8,4,8,1536]{4,3,2,1,0:T(8,128)(2,1)}) custom-call(s32[64]{0:T(128)} %iota_select_fusion.source_ref, s32[2,64,1]{2,1,0:T(8,128)} %copy.17.sexp_ref, s32[2,8,1024]{2,1,0:T(8,128)} %bitcast.42, ...), custom_call_target="tpu_custom_call" | custom-call | tf_op jit(solution)/shard_map/pallas_call | solution.py:326
  316.8 0.0 copy-start.2
  316.8 4.8 %copy.18 = bf16[1536,1024]{0,1:T(8,128)(2,1)} copy(bf16[1536,1024]{1,0:T(8,128)(2,1)} %bitcast.37) | data formatting | bytes 6291456 | tf_op jit(solution)/shard_map/reshape | solution.py:371
  321.6 0.0 copy-done.2
  321.6 0.0 copy-start.1
  321.6 1.1 copy.23
  322.7 0.8 copy-done.1
  323.5 0.0 copy-start
  323.5 1.1 copy.24
  324.7 0.8 copy-done
  325.5 1.1 copy.25
  (1 shorter events, 0.0 us)
Async XLA Ops:
  316.8 4.8 %copy-start.2 = (bf16[2,8,4,8,1536]{4,3,2,1,0:T(8,128)(2,1)S(1)}, bf16[2,8,4,8,1536]{4,3,2,1,0:T(8,128)(2,1)}, u32[]{:S(2)}) copy-start(bf16[2,8,4,8,1536]{4,3,2,1,0:T(8,128)(2,1)} %get-tuple-element.9) | copy-start | bytes 4718596
  321.6 2.0 copy-start.1
  323.5 2.0 copy-start

commit v7 on v6

--- a/solution.py
+++ b/solution.py
@@ -218,8 +218,6 @@
     swap1 = swap_weights(1, mine1_ref, other1_ref)
     combine(back0_ref, rank0_ref, gate0_ref, 0)
     await_bytes(back0_ref.at[everything], osend.at[0])
-    await_bytes(held_ref, hrecv)
-    lax.fori_loop(0, all_slots, permute, 0)
 
     def place(i):
         plane = near(2 * (i // (2 * cols)) + lax.rem(i, 2))
@@ -240,9 +238,6 @@
         post(send_ref.at[block + cols], rows1_ref.at[me], 2 * plane + 1, column, osend.at[1], orecv.at[1, here])
 
     choose(0)
-    for to_core in range(2):
-        send_moves(0, to_core)
-        send_moves(1, to_core)
 
     def step(i, carry):
         choose(i)
@@ -252,11 +247,13 @@
     lax.fori_loop(1, all_slots, step, 0)
     swap1.wait_recv()
     ship(all_slots - 1)
+    await_bytes(held_ref, hrecv)
+    lax.fori_loop(0, all_slots, permute, 0)
     acc_ref[...] = hid_ref[...].astype(F32)
     experts(True, rows1_ref, mine1_ref, other1_ref, back1_ref, 2)
     for to_core in range(2):
-        send_moves(2, to_core)
-        send_moves(3, to_core)
+        for i in range(planes):
+            send_moves(i, to_core)
     combine(back1_ref, rank1_ref, gate1_ref, 2)
 
     z, y = tp // side, lax.rem(tp, side)

time: 329 us -> 296 us (0.90)
  Pallas kernels: 310 us -> 276 us
    pallas_call x1, Pallas kernels: 310 us -> 276 us  [run_layers(): pl.pallas_call(functools.partial(layers_kernel, group, cols, side, cap),...]
where the time goes in v7:
time: 296 us; the launch traced here: 292 us
  Pallas kernels  276 us (93%)
  local copies, waits for them, and re-layouts  13.3 us (4%)
    pallas_call x1, Pallas kernels, run_layers(): pl.pallas_call(functools.partial(layers_kernel, group, cols, side, cap),...  276 us

profile of v7, /device:TPU:1, one launch (start us, length us, event | category | flops | bytes accessed | tf_op | source)
XLA Modules:
  0.0 292.5 jit_solution(17546184866116955432)
XLA Ops:
  0.7 0.7 fusion.1
  1.4 0.1 select_reduce_fusion
  1.5 0.1 fusion
  1.5 0.5 iota_select_fusion.source_ref
  2.1 0.9 and_reduce_fusion
  3.0 0.7 select_bitcast_fusion
  3.7 0.7 copy.17.sexp_ref
  4.4 1.2 constant_dynamic-slice_fusion
  5.6 0.8 copy.19
  6.4 276.2 %shard_map.120 = (bf16[4,4,96,1024]{3,2,1,0:T(8,128)(2,1)}, bf16[2,8,4,8,1536]{4,3,2,1,0:T(8,128)(2,1)}, bf16[2,8,4,8,1536]{4,3,2,1,0:T(8,128)(2,1)}, bf16[2,8,4,8,1536]{4,3,2,1,0:T(8,128)(2,1)}) custom-call(s32[64]{0:T(128)} %iota_select_fusion.source_ref, s32[2,64,1]{2,1,0:T(8,128)} %copy.17.sexp_ref, s32[2,8,1024]{2,1,0:T(8,128)} %bitcast.42, ...), custom_call_target="tpu_custom_call" | custom-call | tf_op jit(solution)/shard_map/pallas_call | solution.py:323
  282.6 0.0 copy-start.2
  282.6 4.8 %copy.18 = bf16[1536,1024]{0,1:T(8,128)(2,1)} copy(bf16[1536,1024]{1,0:T(8,128)(2,1)} %bitcast.37) | data formatting | bytes 6291456 | tf_op jit(solution)/shard_map/reshape | solution.py:368
  287.4 0.0 copy-done.2
  287.4 0.0 copy-start.1
  287.4 1.1 copy.23
  288.5 0.8 copy-done.1
  289.4 0.0 copy-start
  289.4 1.1 copy.24
  290.5 0.8 copy-done
  291.3 1.1 copy.25
  (1 shorter events, 0.0 us)
Async XLA Ops:
  282.6 4.8 %copy-start.2 = (bf16[2,8,4,8,1536]{4,3,2,1,0:T(8,128)(2,1)S(1)}, bf16[2,8,4,8,1536]{4,3,2,1,0:T(8,128)(2,1)}, u32[]{:S(2)}) copy-start(bf16[2,8,4,8,1536]{4,3,2,1,0:T(8,128)(2,1)} %get-tuple-element.9) | copy-start | bytes 4718596
  287.4 2.0 copy-start.1
  289.4 2.0 copy-start

commit v8 on v7

--- a/solution.py
+++ b/solution.py
@@ -209,12 +209,12 @@
     send_weights(0, mine0_ref)
     lax.fori_loop(0, group, send_rows, 0)
     send_weights(1, mine1_ref)
-    lax.fori_loop(0, group, gather_moves, 0)
     table(1, rank1_ref, gate1_ref)
     acc_ref[...] = res_ref[...].astype(F32)
     swap0 = swap_weights(0, mine0_ref, other0_ref)
     swap0.wait_recv()
     experts(False, rows0_ref, mine0_ref, other0_ref, back0_ref, 0)
+    lax.fori_loop(0, group, gather_moves, 0)
     swap1 = swap_weights(1, mine1_ref, other1_ref)
     combine(back0_ref, rank0_ref, gate0_ref, 0)
     await_bytes(back0_ref.at[everything], osend.at[0])

time: 296 us -> 343 us (1.16)
  the two profiles are of different devices: /device:TPU:1 before, /device:TPU:31 now
where the time goes in v8:
time: 343 us
  Pallas kernels  327 us (95%)
  local copies, waits for them, and re-layouts  13.3 us (4%)
    pallas_call x1, Pallas kernels, run_layers(): pl.pallas_call(functools.partial(layers_kernel, group, cols, side, cap),...  327 us

profile of v8, /device:TPU:31, one launch (start us, length us, event | category | flops | bytes accessed | tf_op | source)
XLA Modules:
  0.0 343.0 jit_solution(12547379164992232016)
XLA Ops:
  0.7 0.7 fusion.1
  1.4 0.1 select_reduce_fusion
  1.5 0.1 fusion
  1.5 0.5 iota_select_fusion.source_ref
  2.1 0.9 and_reduce_fusion
  3.0 0.7 select_bitcast_fusion
  3.7 0.7 copy.17.sexp_ref
  4.4 1.2 constant_dynamic-slice_fusion
  5.6 0.8 copy.19
  6.4 326.7 %shard_map.120 = (bf16[4,4,96,1024]{3,2,1,0:T(8,128)(2,1)}, bf16[2,8,4,8,1536]{4,3,2,1,0:T(8,128)(2,1)}, bf16[2,8,4,8,1536]{4,3,2,1,0:T(8,128)(2,1)}, bf16[2,8,4,8,1536]{4,3,2,1,0:T(8,128)(2,1)}) custom-call(s32[64]{0:T(128)} %iota_select_fusion.source_ref, s32[2,64,1]{2,1,0:T(8,128)} %copy.17.sexp_ref, s32[2,8,1024]{2,1,0:T(8,128)} %bitcast.42, ...), custom_call_target="tpu_custom_call" | custom-call | tf_op jit(solution)/shard_map/pallas_call | solution.py:323
  333.1 0.0 copy-start.2
  333.2 4.8 %copy.18 = bf16[1536,1024]{0,1:T(8,128)(2,1)} copy(bf16[1536,1024]{1,0:T(8,128)(2,1)} %bitcast.37) | data formatting | bytes 6291456 | tf_op jit(solution)/shard_map/reshape | solution.py:368
  337.9 0.0 copy-done.2
  337.9 0.0 copy-start.1
  337.9 1.1 copy.23
  339.1 0.8 copy-done.1
  339.9 0.0 copy-start
  339.9 1.1 copy.24
  341.0 0.8 copy-done
  341.9 1.1 copy.25
  (1 shorter events, 0.0 us)
Async XLA Ops:
  333.1 4.8 %copy-start.2 = (bf16[2,8,4,8,1536]{4,3,2,1,0:T(8,128)(2,1)S(1)}, bf16[2,8,4,8,1536]{4,3,2,1,0:T(8,128)(2,1)}, u32[]{:S(2)}) copy-start(bf16[2,8,4,8,1536]{4,3,2,1,0:T(8,128)(2,1)} %get-tuple-element.9) | copy-start | bytes 4718596
  337.9 2.0 copy-start.1
  339.9 2.0 copy-start
